TPU v7x, 32 devices: a whole 2x2x4 slice. The times are simulated.
32 devices in a mesh: gx: 8 (over z, x), gy: 4 (over y, core).
Axes of the slice: x: 2, y: 2, z: 4, core: 2. Of those that a mesh axis runs over, the one named last changes fastest.
Arguments:
- probe_seeds: int32 [4], replicated, may hold values from 0 to 1048575
- damping: float32 [512, 1024], P('gx', 'gy'), may hold values from 0.2 to 1
- coupling_x: float32 [512, 1024], P('gx', 'gy'), may hold values from 0.05 to 0.5
- coupling_y: float32 [512, 1024], P('gx', 'gy'), may hold values from 0.05 to 0.5
- sensor_count: int32 [8, 4], P('gx', 'gy'), may hold values from 1 to 256, as said below
- sensor_cells: int32 [8, 4, 256], P('gx', 'gy'), may hold values from 0 to 16383
- obs_weight: float32 [8, 4, 256, 256], P('gx', 'gy'), as said below
Outputs:
- solution: float32 [4, 512, 1024], P(None, 'gx', 'gy')
- trace_estimate: float32 [], replicated
Inputs may be any that keep to these rules, and one draw needn't show every extreme that they name: `sensor_count`: at most 256, and some block has exactly 256 in every draw; blocks near a few cluster centres are far busier than the rest. `sensor_cells`: cells within the block, numbered row by row. `obs_weight`: each block's matrix is symmetric positive definite.
All inputs are finite; a program needn't handle non-finite values.
Results may differ from a plain program's by a relative error of at most 0.0003.
Values sent between devices are 32-bit elements; how exact they have to be, the bound alone decides.
No kernel may reach another device: no remote copies, remote signals or barrier semaphores. Data moves between devices by JAX's collectives and lax.ppermute only.
A program may use at most 64 MiB of HBM per device.

v0:
```python
import jax
import jax.numpy as jnp
from jax import lax
from jax.sharding import PartitionSpec as P


def with_halo(cells, sides, width):
    for axis, dim in sides:
        count = lax.axis_size(axis)
        head = lax.slice_in_dim(cells, 0, width, axis=dim)
        tail = lax.slice_in_dim(cells, cells.shape[dim] - width, cells.shape[dim], axis=dim)
        cells = jnp.concatenate(
            [
                lax.ppermute(tail, axis, [(i, (i + 1) % count) for i in range(count)]),
                cells,
                lax.ppermute(head, axis, [((i + 1) % count, i) for i in range(count)]),
            ],
            axis=dim,
        )
    return cells


def shifted(value, axis, steps):
    count = lax.axis_size(axis)
    pairs = [(source, (source + steps) % count) for source in range(count)]
    return lax.ppermute(value, axis, pairs)


def rademacher(seeds, row_ids, col_ids):
    mixed = (
        seeds[:, None, None] * 668265261
        + row_ids[None, :, None] * 374761393
        + col_ids[None, None, :] * 1103515245
    )
    mixed = (mixed ^ mixed >> 16 & 65535) * 73244475
    mixed = (mixed ^ mixed >> 16 & 65535) * 73244475
    mixed = mixed ^ mixed >> 16 & 65535
    bit_value = mixed >> 7 & 1
    return (2 * bit_value - 1).astype(jnp.float32)


def apply_region(padded, damping, face_rows, face_cols):
    centre = padded[:, 1:-1, 1:-1]
    return (
        damping * centre
        + face_rows[1:] * (centre - padded[:, 2:, 1:-1])
        + face_rows[:-1] * (centre - padded[:, :-2, 1:-1])
        + face_cols[:, 1:] * (centre - padded[:, 1:-1, 2:])
        + face_cols[:, :-1] * (centre - padded[:, 1:-1, :-2])
    )


def rim_one(field):
    return with_halo(field, (("gx", 1), ("gy", 2)), 1)


def curvature(first, second):
    return lax.psum(jnp.sum(first * second, axis=(1, 2)), ("gx", "gy"))


def per_device(
    probe_seeds, damping, coupling_x, coupling_y, sensor_count, sensor_cells, obs_weight
):
    block_rows, block_cols = damping.shape
    row_ids = lax.axis_index("gx") * block_rows + jnp.arange(block_rows, dtype=jnp.int32)
    col_ids = lax.axis_index("gy") * block_cols + jnp.arange(block_cols, dtype=jnp.int32)
    probes = rademacher(probe_seeds, row_ids, col_ids)
    before_rows = shifted(coupling_x[-1:, :], "gx", 1)
    before_cols = shifted(coupling_y[:, -1:], "gy", 1)
    inner = (
        damping,
        jnp.concatenate([before_rows, coupling_x], 0),
        jnp.concatenate([before_cols, coupling_y], 1),
    )
    count = sensor_count[0, 0]
    cell_ids = sensor_cells[0, 0]
    weight = obs_weight[0, 0]
    mask = (jnp.arange(weight.shape[0]) < count).astype(jnp.float32)

    def observe(field):
        flat = field.reshape(field.shape[0], -1)
        sampled = jnp.take(flat, cell_ids, axis=1) * mask
        weighted = jnp.dot(sampled, weight, precision=lax.Precision.HIGHEST)
        weighted = weighted * mask
        return jnp.zeros_like(flat).at[:, cell_ids].add(weighted).reshape(field.shape)

    def operator_twice(field):
        once = apply_region(rim_one(field), *inner)
        return apply_region(rim_one(once), *inner)

    def hessian(field):
        return operator_twice(field) + observe(field)

    cells_total = block_rows * block_cols * lax.axis_size("gx") * lax.axis_size("gy")
    norm_start = jnp.full((probes.shape[0],), float(cells_total), jnp.float32)
    image = hessian(probes)
    first_step = norm_start / curvature(probes, image)
    solution = first_step[:, None, None] * probes
    residual = probes - first_step[:, None, None] * image
    residual_image = hessian(residual)
    norm_next, product = lax.psum(
        (
            jnp.sum(residual * residual, axis=(1, 2)),
            jnp.sum(residual * residual_image, axis=(1, 2)),
        ),
        ("gx", "gy"),
    )
    ratio = norm_next / norm_start
    direction = residual + ratio[:, None, None] * probes
    second_step = norm_next / (product - ratio * norm_next / first_step)
    solution = solution + second_step[:, None, None] * direction
    total = lax.psum(jnp.sum(probes * solution), ("gx", "gy"))
    return (solution, total / probes.shape[0])


def solution(mesh):
    placed = (
        P(),
        P("gx", "gy"),
        P("gx", "gy"),
        P("gx", "gy"),
        P("gx", "gy"),
        P("gx", "gy", None),
        P("gx", "gy", None, None),
    )
    return jax.shard_map(
        per_device,
        mesh=mesh,
        in_specs=placed,
        out_specs=(P(None, "gx", "gy"), P()),
        check_vma=False,
    )
```

profile of v0, /device:TPU:0, one launch (start us, length us, event | category | flops | bytes accessed | tf_op | source)
XLA Modules:
  0.0 211.1 jit_solution(12646196828088814270)
XLA Ops:
  1.8 6.1 %collective-permute-start = (f32[4,1,256]{2,1,0:T(1,128)S(1)}, f32[4,1,256]{2,1,0:T(1,128)S(1)}, u32[]{:S(2)}, u32[]{:S(2)}) collective-permute-start(f32[4,1,256]{2,1,0:T(1,128)S(1)} %get-tuple-element.26), channel_id=1, source_target_pairs={{4,0},{8,4},{12,8},{16,12},{20,16},{24,20},{28,24},{0,28},{5,1},{9... | collective-permute-start | bytes 12296 | tf_op jit(solution)/shard_map/ppermute | solution.py:16
  11.9 5.1 %copy.25 = f32[4,16384]{0,1:T(8,128)} copy(f32[4,16384]{1,0:T(4,128)S(1)} %add_convert_fusion) | data formatting | bytes 524288 | tf_op jit(solution)/shard_map/convert_element_type | solution.py:39
  16.9 4.1 %gather_fusion = f32[256,4]{1,0:T(8,128)S(1)} fusion(f32[4,16384]{0,1:T(8,128)} %copy.25, s32[1024]{0:T(1024)S(1)} %pad_clamp_fusion), kind=kCustom, calls=%fused_computation.clone | custom fusion | bytes 9216 | tf_op jit(solution)/shard_map/jit(_take)/gather | solution.py:82
  21.4 1.7 collective-permute-start.5
  23.2 2.7 %collective-permute-done.5 = f32[4,66,1]{2,1,0:T(8,128)S(1)} collective-permute-done((f32[4,66,1]{2,1,0:T(8,128)S(1)}, f32[4,66,1]{2,1,0:T(8,128)S(1)}, u32[]{:S(2)}, u32[]{:S(2)}) %collective-permute-start.5) | collective-permute-done | bytes 1088 | tf_op jit(solution)/shard_map/ppermute | solution.py:14
  26.9 4.8 %collective-permute-start.6 = (f32[4,1,256]{2,1,0:T(1,128)S(1)}, f32[4,1,256]{2,1,0:T(1,128)S(1)}, u32[]{:S(2)}, u32[]{:S(2)}) collective-permute-start(f32[4,1,256]{2,1,0:T(1,128)S(1)} %get-tuple-element.24), channel_id=1, source_target_pairs={{4,0},{8,4},{12,8},{16,12},{20,16},{24,20},{28,24},{0,28},{5,1},{9... | collective-permute-start | bytes 12296 | tf_op jit(solution)/shard_map/ppermute | solution.py:16
  33.0 5.0 %collective-permute-done.7 = f32[4,1,256]{2,1,0:T(1,128)S(1)} collective-permute-done((f32[4,1,256]{2,1,0:T(1,128)S(1)}, f32[4,1,256]{2,1,0:T(1,128)S(1)}, u32[]{:S(2)}, u32[]{:S(2)}) %collective-permute-start.7) | collective-permute-done | bytes 4128 | tf_op jit(solution)/shard_map/ppermute | solution.py:14
  38.2 1.7 collective-permute-start.8
  40.1 5.1 %scatter_custom_fusion = f32[4,16384]{0,1:T(8,128)} fusion(s32[256]{0:T(256)S(1)} %bitcast.37, f32[256,4]{1,0:T(8,128)S(1)} %copy.27, f32[]{:T(128)} %constant.53.clone.1), kind=kCustom, calls=%fused_computation.6 | custom fusion | flops 1024 | bytes 262148 | tf_op jit(solution)/shard_map/scatter-add | solution.py:85
  45.2 5.2 %copy.28 = f32[4,64,256]{2,1,0:T(8,128)S(1)} copy(f32[4,64,256]{0,2,1:T(8,128)} %bitcast.31) | data formatting | bytes 524288 | tf_op jit(solution)/shard_map/reshape | solution.py:85
  51.0 36.9 %psum.28 = f32[4]{0:T(128)S(1)} all-reduce(f32[4]{0:T(128)S(1)} %get-tuple-element.9), channel_id=1, replica_groups=mesh['gx'=8,'gy'=4] {'gx','gy'}, use_global_device_ids=true, to_apply=%region_2.4 | all-reduce | flops 4 | bytes 32 | tf_op jit(solution)/shard_map/psum | solution.py:58
  88.2 4.0 %collective-permute-start.10 = (f32[4,1,256]{2,1,0:T(1,128)S(1)}, f32[4,1,256]{2,1,0:T(1,128)S(1)}, u32[]{:S(2)}, u32[]{:S(2)}) collective-permute-start(f32[4,1,256]{2,1,0:T(1,128)S(1)} %get-tuple-element.22), channel_id=1, source_target_pairs={{4,0},{8,4},{12,8},{16,12},{20,16},{24,20},{28,24},{0,28},{5,1},{9... | collective-permute-start | bytes 12296 | tf_op jit(solution)/shard_map/ppermute | solution.py:16
  92.2 1.3 collective-permute-done.10
  93.6 5.0 %collective-permute-done.11 = f32[4,1,256]{2,1,0:T(1,128)S(1)} collective-permute-done((f32[4,1,256]{2,1,0:T(1,128)S(1)}, f32[4,1,256]{2,1,0:T(1,128)S(1)}, u32[]{:S(2)}, u32[]{:S(2)}) %collective-permute-start.11) | collective-permute-done | bytes 4128 | tf_op jit(solution)/shard_map/ppermute | solution.py:14
  98.7 1.7 collective-permute-start.12
  100.5 2.8 %collective-permute-done.13 = f32[4,66,1]{2,1,0:T(8,128)S(1)} collective-permute-done((f32[4,66,1]{2,1,0:T(8,128)S(1)}, f32[4,66,1]{2,1,0:T(8,128)S(1)}, u32[]{:S(2)}, u32[]{:S(2)}) %collective-permute-start.13) | collective-permute-done | bytes 1088 | tf_op jit(solution)/shard_map/ppermute | solution.py:14
  104.3 2.0 collective-permute-start.15
  106.3 4.6 %copy.29 = f32[4,64,256]{0,2,1:T(8,128)} copy(f32[4,64,256]{2,1,0:T(8,128)S(1)} %get-tuple-element.8) | data formatting | bytes 524288 | tf_op jit(solution)/shard_map/sub | solution.py:99
  111.0 4.1 %gather_fusion.1 = f32[256,4]{1,0:T(8,128)S(1)} fusion(f32[4,16384]{0,1:T(8,128)} %bitcast.32, s32[1024]{0:T(1024)S(1)} %pad_clamp_fusion), kind=kCustom, calls=%fused_computation.1.clone | custom fusion | bytes 9216 | tf_op jit(solution)/shard_map/jit(_take)/gather | solution.py:82
  117.5 5.1 %scatter_custom_fusion.1 = f32[4,16384]{0,1:T(8,128)} fusion(s32[256]{0:T(256)S(1)} %bitcast.38, f32[256,4]{1,0:T(8,128)S(1)} %copy.31, f32[]{:T(128)} %constant.53.clone.1), kind=kCustom, calls=%fused_computation.4 | custom fusion | flops 1024 | bytes 262148 | tf_op jit(solution)/shard_map/scatter-add | solution.py:85
  122.6 5.2 %copy.32 = f32[4,64,256]{2,1,0:T(8,128)S(1)} copy(f32[4,64,256]{0,2,1:T(8,128)} %bitcast.30) | data formatting | bytes 524288 | tf_op jit(solution)/shard_map/reshape | solution.py:85
  128.2 38.3 %all-reduce = (f32[4]{0:T(128)S(1)}, f32[4]{0:T(128)S(1)}) all-reduce(f32[4]{0:T(128)S(1)} %get-tuple-element.7, f32[4]{0:T(128)S(1)} %fusion.17), channel_id=1, replica_groups=mesh['gx'=8,'gy'=4] {'gx','gy'}, use_global_device_ids=true, to_apply=%region_4.6 | all-reduce | flops 8 | bytes 64 | tf_op jit(solution)/shard_map/psum | solution.py:101
  166.5 1.6 multiply_reduce_fusion
  168.1 41.2 %psum.31 = f32[]{:T(128)} all-reduce(f32[]{:T(128)} %get-tuple-element.5), channel_id=1, replica_groups=mesh['gx'=8,'gy'=4] {'gx','gy'}, use_global_device_ids=true, to_apply=%region_9.11 | all-reduce | flops 1 | bytes 8 | tf_op jit(solution)/shard_map/psum | solution.py:112
  (76 shorter events, 12.3 us)
Async XLA Ops:
  0.6 31.1 %copy-start = (f32[1,1,256,256]{3,2,1,0:T(8,128)S(1)}, f32[1,1,256,256]{3,2,1,0:T(8,128)}, u32[]{:S(2)}) copy-start(f32[1,1,256,256]{3,2,1,0:T(8,128)} %param.15) | copy-start | bytes 786436
  0.6 20.5 %copy-start.1 = (f32[64,256]{1,0:T(8,128)S(1)}, f32[64,256]{1,0:T(8,128)}, u32[]{:S(2)}) copy-start(f32[64,256]{1,0:T(8,128)} %param.12) | copy-start | bytes 196612
  0.7 22.6 %copy-start.2 = (f32[64,256]{1,0:T(8,128)S(1)}, f32[64,256]{1,0:T(8,128)}, u32[]{:S(2)}) copy-start(f32[64,256]{1,0:T(8,128)} %param.11) | copy-start | bytes 196612
  0.7 39.3 %copy-start.4 = (s32[1,1,256]{2,1,0:T(1,128)S(1)}, s32[1,1,256]{2,1,0:T(1,128)}, u32[]{:S(2)}) copy-start(s32[1,1,256]{2,1,0:T(1,128)} %param.14) | copy-start | bytes 3076
  0.7 25.9 %copy-start.3 = (f32[64,256]{1,0:T(8,128)S(1)}, f32[64,256]{1,0:T(8,128)}, u32[]{:S(2)}) copy-start(f32[64,256]{1,0:T(8,128)} %param.10) | copy-start | bytes 196612
  1.8 19.5 %collective-permute-start = (f32[4,1,256]{2,1,0:T(1,128)S(1)}, f32[4,1,256]{2,1,0:T(1,128)S(1)}, u32[]{:S(2)}, u32[]{:S(2)}) collective-permute-start(f32[4,1,256]{2,1,0:T(1,128)S(1)} %get-tuple-element.26), channel_id=1, source_target_pairs={{4,0},{8,4},{12,8},{16,12},{20,16},{24,20},{28,24},{0,28},{5,1},{9... | collective-permute-start | bytes 12296 | tf_op jit(solution)/shard_map/ppermute | solution.py:16
  7.8 13.4 %collective-permute-start.2 = (f32[4,1,256]{2,1,0:T(1,128)S(1)}, f32[4,1,256]{2,1,0:T(1,128)S(1)}, u32[]{:S(2)}, u32[]{:S(2)}) collective-permute-start(f32[4,1,256]{2,1,0:T(1,128)S(1)} %get-tuple-element.25), channel_id=1, source_target_pairs={{0,4},{4,8},{8,12},{12,16},{16,20},{20,24},{24,28},{28,0},{1,5},{5... | collective-permute-start | bytes 12296 | tf_op jit(solution)/shard_map/ppermute | solution.py:14
  8.6 12.5 %collective-permute-start.4 = (f32[64,1]{1,0:T(8,128)S(1)}, f32[64,1]{1,0:T(8,128)S(1)}, u32[]{:S(2)}, u32[]{:S(2)}) collective-permute-start(f32[64,1]{1,0:T(8,128)S(1)} %slice.138), channel_id=1, source_target_pairs={{0,1},{1,2},{2,3},{3,0},{4,5},{5,6},{6,7},{7,4},{8,9},{9,10},{10,1... | collective-permute-start | bytes 776 | tf_op jit(solution)/shard_map/ppermute | solution.py:26
  9.4 13.9 %collective-permute-start.1 = (f32[1,256]{1,0:T(1,128)S(1)}, f32[1,256]{1,0:T(1,128)S(1)}, u32[]{:S(2)}, u32[]{:S(2)}) collective-permute-start(f32[1,256]{1,0:T(1,128)S(1)} %slice.132), channel_id=1, source_target_pairs={{0,4},{4,8},{8,12},{12,16},{16,20},{20,24},{24,28},{28,0},{1,5},{5... | collective-permute-start | bytes 3080 | tf_op jit(solution)/shard_map/ppermute | solution.py:26
  21.4 4.6 %collective-permute-start.5 = (f32[4,66,1]{2,1,0:T(8,128)S(1)}, f32[4,66,1]{2,1,0:T(8,128)S(1)}, u32[]{:S(2)}, u32[]{:S(2)}) collective-permute-start(f32[4,66,1]{2,1,0:T(8,128)S(1)} %get-tuple-element.18), channel_id=1, source_target_pairs={{0,1},{1,2},{2,3},{3,0},{4,5},{5,6},{6,7},{7,4},{8,9},{9,10},{10,1... | collective-permute-start | bytes 3176 | tf_op jit(solution)/shard_map/ppermute | solution.py:14
  23.1 3.6 %collective-permute-start.3 = (f32[4,66,1]{2,1,0:T(8,128)S(1)}, f32[4,66,1]{2,1,0:T(8,128)S(1)}, u32[]{:S(2)}, u32[]{:S(2)}) collective-permute-start(f32[4,66,1]{2,1,0:T(8,128)S(1)} %get-tuple-element.17), channel_id=1, source_target_pairs={{1,0},{2,1},{3,2},{0,3},{5,4},{6,5},{7,6},{4,7},{9,8},{10,9},{11,1... | collective-permute-start | bytes 3176 | tf_op jit(solution)/shard_map/ppermute | solution.py:16
  26.9 6.1 %collective-permute-start.6 = (f32[4,1,256]{2,1,0:T(1,128)S(1)}, f32[4,1,256]{2,1,0:T(1,128)S(1)}, u32[]{:S(2)}, u32[]{:S(2)}) collective-permute-start(f32[4,1,256]{2,1,0:T(1,128)S(1)} %get-tuple-element.24), channel_id=1, source_target_pairs={{4,0},{8,4},{12,8},{16,12},{20,16},{24,20},{28,24},{0,28},{5,1},{9... | collective-permute-start | bytes 12296 | tf_op jit(solution)/shard_map/ppermute | solution.py:16
  31.7 6.3 %collective-permute-start.7 = (f32[4,1,256]{2,1,0:T(1,128)S(1)}, f32[4,1,256]{2,1,0:T(1,128)S(1)}, u32[]{:S(2)}, u32[]{:S(2)}) collective-permute-start(f32[4,1,256]{2,1,0:T(1,128)S(1)} %get-tuple-element.23), channel_id=1, source_target_pairs={{0,4},{4,8},{8,12},{12,16},{16,20},{20,24},{24,28},{28,0},{1,5},{5... | collective-permute-start | bytes 12296 | tf_op jit(solution)/shard_map/ppermute | solution.py:14
  38.1 12.3 %collective-permute-start.9 = (f32[4,66,1]{2,1,0:T(8,128)S(1)}, f32[4,66,1]{2,1,0:T(8,128)S(1)}, u32[]{:S(2)}, u32[]{:S(2)}) collective-permute-start(f32[4,66,1]{2,1,0:T(8,128)S(1)} %get-tuple-element.16), channel_id=1, source_target_pairs={{0,1},{1,2},{2,3},{3,0},{4,5},{5,6},{6,7},{7,4},{8,9},{9,10},{10,1... | collective-permute-start | bytes 3176 | tf_op jit(solution)/shard_map/ppermute | solution.py:14
  38.2 12.3 %collective-permute-start.8 = (f32[4,66,1]{2,1,0:T(8,128)S(1)}, f32[4,66,1]{2,1,0:T(8,128)S(1)}, u32[]{:S(2)}, u32[]{:S(2)}) collective-permute-start(f32[4,66,1]{2,1,0:T(8,128)S(1)} %get-tuple-element.15), channel_id=1, source_target_pairs={{1,0},{2,1},{3,2},{0,3},{5,4},{6,5},{7,6},{4,7},{9,8},{10,9},{11,1... | collective-permute-start | bytes 3176 | tf_op jit(solution)/shard_map/ppermute | solution.py:16
  88.2 5.4 %collective-permute-start.10 = (f32[4,1,256]{2,1,0:T(1,128)S(1)}, f32[4,1,256]{2,1,0:T(1,128)S(1)}, u32[]{:S(2)}, u32[]{:S(2)}) collective-permute-start(f32[4,1,256]{2,1,0:T(1,128)S(1)} %get-tuple-element.22), channel_id=1, source_target_pairs={{4,0},{8,4},{12,8},{16,12},{20,16},{24,20},{28,24},{0,28},{5,1},{9... | collective-permute-start | bytes 12296 | tf_op jit(solution)/shard_map/ppermute | solution.py:16
  92.2 6.3 %collective-permute-start.11 = (f32[4,1,256]{2,1,0:T(1,128)S(1)}, f32[4,1,256]{2,1,0:T(1,128)S(1)}, u32[]{:S(2)}, u32[]{:S(2)}) collective-permute-start(f32[4,1,256]{2,1,0:T(1,128)S(1)} %get-tuple-element.21), channel_id=1, source_target_pairs={{0,4},{4,8},{8,12},{12,16},{16,20},{20,24},{24,28},{28,0},{1,5},{5... | collective-permute-start | bytes 12296 | tf_op jit(solution)/shard_map/ppermute | solution.py:14
  98.7 4.6 %collective-permute-start.13 = (f32[4,66,1]{2,1,0:T(8,128)S(1)}, f32[4,66,1]{2,1,0:T(8,128)S(1)}, u32[]{:S(2)}, u32[]{:S(2)}) collective-permute-start(f32[4,66,1]{2,1,0:T(8,128)S(1)} %get-tuple-element.14), channel_id=1, source_target_pairs={{0,1},{1,2},{2,3},{3,0},{4,5},{5,6},{6,7},{7,4},{8,9},{9,10},{10,1... | collective-permute-start | bytes 3176 | tf_op jit(solution)/shard_map/ppermute | solution.py:14
  98.7 5.2 %collective-permute-start.12 = (f32[4,66,1]{2,1,0:T(8,128)S(1)}, f32[4,66,1]{2,1,0:T(8,128)S(1)}, u32[]{:S(2)}, u32[]{:S(2)}) collective-permute-start(f32[4,66,1]{2,1,0:T(8,128)S(1)} %get-tuple-element.13), channel_id=1, source_target_pairs={{1,0},{2,1},{3,2},{0,3},{5,4},{6,5},{7,6},{4,7},{9,8},{10,9},{11,1... | collective-permute-start | bytes 3176 | tf_op jit(solution)/shard_map/ppermute | solution.py:16
  104.3 10.9 %collective-permute-start.14 = (f32[4,1,256]{2,1,0:T(1,128)S(1)}, f32[4,1,256]{2,1,0:T(1,128)S(1)}, u32[]{:S(2)}, u32[]{:S(2)}) collective-permute-start(f32[4,1,256]{2,1,0:T(1,128)S(1)} %get-tuple-element.20), channel_id=1, source_target_pairs={{4,0},{8,4},{12,8},{16,12},{20,16},{24,20},{28,24},{0,28},{5,1},{9... | collective-permute-start | bytes 12296 | tf_op jit(solution)/shard_map/ppermute | solution.py:16
  104.3 10.8 %collective-permute-start.15 = (f32[4,1,256]{2,1,0:T(1,128)S(1)}, f32[4,1,256]{2,1,0:T(1,128)S(1)}, u32[]{:S(2)}, u32[]{:S(2)}) collective-permute-start(f32[4,1,256]{2,1,0:T(1,128)S(1)} %get-tuple-element.19), channel_id=1, source_target_pairs={{0,4},{4,8},{8,12},{12,16},{16,20},{20,24},{24,28},{28,0},{1,5},{5... | collective-permute-start | bytes 12296 | tf_op jit(solution)/shard_map/ppermute | solution.py:14
  115.3 12.6 %collective-permute-start.17 = (f32[4,66,1]{2,1,0:T(8,128)S(1)}, f32[4,66,1]{2,1,0:T(8,128)S(1)}, u32[]{:S(2)}, u32[]{:S(2)}) collective-permute-start(f32[4,66,1]{2,1,0:T(8,128)S(1)} %get-tuple-element.12), channel_id=1, source_target_pairs={{0,1},{1,2},{2,3},{3,0},{4,5},{5,6},{6,7},{7,4},{8,9},{9,10},{10,1... | collective-permute-start | bytes 3176 | tf_op jit(solution)/shard_map/ppermute | solution.py:14
  115.8 12.1 %collective-permute-start.16 = (f32[4,66,1]{2,1,0:T(8,128)S(1)}, f32[4,66,1]{2,1,0:T(8,128)S(1)}, u32[]{:S(2)}, u32[]{:S(2)}) collective-permute-start(f32[4,66,1]{2,1,0:T(8,128)S(1)} %get-tuple-element.11), channel_id=1, source_target_pairs={{1,0},{2,1},{3,2},{0,3},{5,4},{6,5},{7,6},{4,7},{9,8},{10,9},{11,1... | collective-permute-start | bytes 3176 | tf_op jit(solution)/shard_map/ppermute | solution.py:16
where the time goes:
time: 212 us; the launch traced here: 211 us
  blocking collectives  116 us (55%)
  local copies, waits for them, and re-layouts  31 us (15%)
  starting transfers between devices  24.2 us (11%)
  waiting for transfers between devices  19.3 us (9%)
  other arithmetic  16.5 us (8%)
  between operations  3.4 us (2%)
    psum x1, blocking collectives, per_device(): total = lax.psum(jnp.sum(probes * solution), ('gx', 'gy'))  41.2 us
    psum x1, blocking collectives, per_device(): lax.psum((jnp.sum(residual * residual, axis=(1, 2)), jnp.sum(residual * r...  38.3 us
    psum x1, blocking collectives, curvature(): return lax.psum(jnp.sum(first * second, axis=(1, 2)), ('gx', 'gy'))  36.9 us
    ppermute x8, starting transfers between devices, with_halo(): lax.ppermute(head, axis, [((i + 1) % count, i) for i in range(count)])  19.9 us
    ppermute x8, waiting for transfers between devices, with_halo(): lax.ppermute(tail, axis, [(i, (i + 1) % count) for i in range(count)])  15.5 us
    reshape x2, local copies, waits for them, and re-layouts, observe(): jnp.zeros_like(flat).at[:, cell_ids].add(weighted).reshape(field.shape)  10.5 us
    scatter-add x2, other arithmetic, observe(): jnp.zeros_like(flat).at[:, cell_ids].add(weighted).reshape(field.shape)  10.3 us
    gather x4, local copies, waits for them, and re-layouts, observe(): sampled = jnp.take(flat, cell_ids, axis=1) * mask  8.35 us
  transfers between devices with their start and end apart: 18, of which 8 were waited for; matrix products, arithmetic and copies ran while one was open for 20% of the time, Pallas kernels for 0%

commit v1 on v0

v1 whole, which is shorter than its diff:
```python
import jax
import jax.numpy as jnp
from jax import lax
from jax.experimental import pallas as pl
from jax.experimental.pallas import tpu as pltpu
from jax.sharding import PartitionSpec as P

LANES = 128
SUBS = 8
F32 = jnp.float32
BF16 = jnp.bfloat16
VMEM = pl.BlockSpec(memory_space=pltpu.VMEM)
SMEM = pl.BlockSpec(memory_space=pltpu.SMEM)


def shifted(value, axis, steps):
    count = lax.axis_size(axis)
    pairs = [(source, (source + steps) % count) for source in range(count)]
    return lax.ppermute(value, axis, pairs)


def sign_bits(seeds, row_ids, col_ids):
    mixed = seeds * 668265261 + row_ids * 374761393 + col_ids * 1103515245
    mixed = (mixed ^ ((mixed >> 16) & 65535)) * 73244475
    mixed = (mixed ^ ((mixed >> 16) & 65535)) * 73244475
    mixed = mixed ^ ((mixed >> 16) & 65535)
    return (2 * ((mixed >> 7) & 1) - 1).astype(F32)


def iota(shape, dim):
    return lax.broadcasted_iota(jnp.int32, shape, dim)


def roll(value, steps, dim):
    return pltpu.roll(value, steps % value.shape[dim], dim)


def pieces(value):
    high = value.astype(BF16)
    rest = value - high.astype(F32)
    middle = rest.astype(BF16)
    low = (rest - middle.astype(F32)).astype(BF16)
    return high, middle, low


def split_cells(cells, block_cols):
    rows = jnp.floor((cells.astype(F32) + 0.5) * (1.0 / block_cols)).astype(jnp.int32)
    return rows, cells - rows * block_cols


def one_hots(cells, block_rows, block_cols):
    rows, cols = split_cells(cells, block_cols)
    slots = cells.shape[1]
    row_hot = jnp.where(iota((block_rows, slots), 0) == rows, 1.0, 0.0)
    col_hot = jnp.where(iota((block_cols, slots), 0) == cols, 1.0, 0.0).astype(BF16)
    return row_hot, col_hot


def side_pack_kernel(d_ref, cx_ref, cy_ref, left_ref, right_ref):
    block_rows, block_cols = d_ref.shape
    lane = iota((block_rows, LANES), 1)
    first = slice(0, LANES)
    last = slice(block_cols - LANES, block_cols)
    left_ref[...] = jnp.where(
        lane < 3,
        cy_ref[:, first],
        jnp.where(lane < 6, roll(d_ref[:, first], 3, 1), roll(cx_ref[:, first], 6, 1)),
    )
    right_ref[...] = jnp.where(
        lane >= LANES - 3,
        cy_ref[:, last],
        jnp.where(lane >= LANES - 6, roll(d_ref[:, last], -3, 1), roll(cx_ref[:, last], -6, 1)),
    )


def side_tiles(from_right, from_left):
    near_right = iota(from_right.shape, 1) < LANES // 2
    cy = jnp.where(near_right, from_right, from_left)
    d = jnp.where(near_right, roll(from_right, -3, 1), roll(from_left, 3, 1))
    cx = jnp.where(near_right, roll(from_right, -6, 1), roll(from_left, 6, 1))
    return d, cx, cy


def observe_kernel(
    seeds_ref, count_ref, cells_ref, weight_ref, probes_ref, obs_ref, left_ref, right_ref
):
    count, wide_rows, wide_cols = probes_ref.shape
    _, block_rows, block_cols = obs_ref.shape
    row_start = lax.axis_index("gx") * block_rows
    col_start = lax.axis_index("gy") * block_cols
    rows_total = lax.axis_size("gx") * block_rows
    cols_total = lax.axis_size("gy") * block_cols

    slots = cells_ref.shape[1]
    cells = cells_ref[...]
    rows, cols = split_cells(cells, block_cols)
    padded = max(SUBS, count)
    which = iota((padded, slots), 0)
    seeds = jnp.zeros((padded, slots), jnp.int32)
    for k in range(count):
        seeds = jnp.where(which == k, seeds_ref[k], seeds)
    live = jnp.where(iota((1, slots), 1) < count_ref[0, 0], 1.0, 0.0)
    sampled = sign_bits(seeds, rows + row_start, cols + col_start) * live
    weighted = (
        jnp.dot(sampled, weight_ref[...], precision=lax.Precision.HIGHEST, preferred_element_type=F32)
        * live
    )
    row_hot, col_hot = one_hots(cells, block_rows, block_cols)
    parts = pieces(weighted)
    stack = [
        (row_hot * part[k : k + 1].astype(F32)).astype(BF16) for k in range(count) for part in parts
    ]
    spread = lax.dot_general(
        jnp.concatenate(stack, 0), col_hot, (((1,), (1,)), ((), ())), preferred_element_type=F32
    )
    lane = iota((block_rows, LANES), 1)
    left = jnp.zeros((block_rows, LANES), F32)
    right = jnp.zeros((block_rows, LANES), F32)
    for k in range(count):
        base = 3 * k * block_rows
        high, middle, low = (
            spread[base + i * block_rows : base + (i + 1) * block_rows] for i in range(3)
        )
        total = (low + middle) + high
        obs_ref[k] = total
        left = jnp.where(lane == k, roll(total[:, :LANES], k, 1), left)
        right = jnp.where(
            lane == LANES - count + k, roll(total[:, block_cols - LANES :], k + 1 - count, 1), right
        )
    left_ref[...] = left
    right_ref[...] = right

    wide = (wide_rows, wide_cols)
    row_ids = iota(wide, 0)
    row_ids = row_start + jnp.where(row_ids >= wide_rows - SUBS, row_ids - wide_rows, row_ids)
    row_ids = jnp.where(row_ids < 0, row_ids + rows_total, row_ids)
    row_ids = jnp.where(row_ids >= rows_total, row_ids - rows_total, row_ids)
    col_ids = iota(wide, 1)
    col_ids = col_start + jnp.where(col_ids >= wide_cols - LANES // 2, col_ids - wide_cols, col_ids)
    col_ids = jnp.where(col_ids < 0, col_ids + cols_total, col_ids)
    col_ids = jnp.where(col_ids >= cols_total, col_ids - cols_total, col_ids)
    for k in range(count):
        probes_ref[k] = sign_bits(seeds_ref[k], row_ids, col_ids)


def edge_pack_kernel(
    d_ref, cx_ref, cy_ref, from_right_ref, from_left_ref, obs_ref, up_ref, down_ref
):
    count, block_rows, block_cols = obs_ref.shape
    wide_cols = block_cols + LANES
    sub = iota((SUBS, wide_cols), 0)
    nothing = jnp.zeros((1, LANES), F32)

    def wide_rows_of(rows):
        sides = side_tiles(from_right_ref[rows], from_left_ref[rows])
        return [
            jnp.concatenate([ref[rows], side], 1)
            for ref, side in zip((d_ref, cx_ref, cy_ref), sides)
        ]

    def observed(row):
        lines = [
            jnp.concatenate([obs_ref[k, row : row + 1], nothing], 1) for k in range(count)
        ]
        spare = -count % SUBS
        return jnp.concatenate(lines + [jnp.zeros((spare, wide_cols), F32)], 0)

    d, cx, cy = wide_rows_of(slice(0, SUBS))
    up_ref[:SUBS] = jnp.where(sub < 2, cx, jnp.where(sub < 4, roll(d, 2, 0), roll(cy, 4, 0)))
    up_ref[SUBS:] = observed(0)
    d, cx, cy = wide_rows_of(slice(block_rows - SUBS, block_rows))
    down_ref[:SUBS] = jnp.where(
        sub >= SUBS - 3, cx, jnp.where(sub >= SUBS - 5, roll(d, -3, 0), roll(cy, -5, 0))
    )
    down_ref[SUBS:] = observed(block_rows - 1)


def stencil(v, coefs):
    centre, cx, cx_before, cy, cy_before = coefs
    return (
        centre[...] * v
        - cx[...] * roll(v, -1, 0)
        - cx_before[...] * roll(v, 1, 0)
        - cy[...] * roll(v, -1, 1)
        - cy_before[...] * roll(v, 1, 1)
    )


def image_kernel(
    count_ref,
    cells_ref,
    weight_ref,
    d_ref,
    cx_ref,
    cy_ref,
    from_right_ref,
    from_left_ref,
    from_below_ref,
    from_above_ref,
    obs_ref,
    obs_right_ref,
    obs_left_ref,
    probes_ref,
    image_ref,
    sums_ref,
    centre,
    cx_wide,
    cx_before,
    cy_wide,
    cy_before,
):
    count, block_rows, block_cols = obs_ref.shape
    own_rows, own_cols = slice(0, block_rows), slice(0, block_cols)
    below, above = slice(block_rows, block_rows + SUBS), slice(block_rows + SUBS, block_rows + 2 * SUBS)
    side = slice(block_cols, block_cols + LANES)
    d_side, cx_side, cy_side = side_tiles(from_right_ref[...], from_left_ref[...])
    low, high = from_below_ref[:SUBS], from_above_ref[:SUBS]
    for target, own, tile, low_steps, high_steps in (
        (centre, d_ref, d_side, -2, 3),
        (cx_wide, cx_ref, cx_side, 0, 0),
        (cy_wide, cy_ref, cy_side, -4, 5),
    ):
        target[own_rows, own_cols] = own[...]
        target[own_rows, side] = tile
        target[below] = roll(low, low_steps, 0) if low_steps else low
        target[above] = roll(high, high_steps, 0) if high_steps else high
    cx, cy = cx_wide[...], cy_wide[...]
    cx_up, cy_left = roll(cx, 1, 0), roll(cy, 1, 1)
    cx_before[...] = cx_up
    cy_before[...] = cy_left
    centre[...] = centre[...] + (cx + cx_up) + (cy + cy_left)
    coefs = (centre, cx_wide, cx_before, cy_wide, cy_before)

    slots = cells_ref.shape[1]
    row_hot, col_hot = one_hots(cells_ref[...], block_rows, block_cols)
    live = jnp.where(iota((1, slots), 1) < count_ref[0, 0], 1.0, 0.0)
    lane = iota((block_rows, LANES), 1)
    sub = iota((SUBS, block_cols + LANES), 0)
    stack, lines = [], []
    for k in range(count):
        probe = probes_ref[k]
        once = stencil(probe, coefs)
        right = jnp.where(lane == 0, roll(obs_right_ref[...], -k, 1), 0.0)
        left = jnp.where(lane == LANES - 1, roll(obs_left_ref[...], count - 1 - k, 1), right)
        under = jnp.where(sub == 0, from_below_ref[SUBS + k : SUBS + k + 1], 0.0)
        over = jnp.where(sub == SUBS - 1, from_above_ref[SUBS + k : SUBS + k + 1], 0.0)
        seen = jnp.concatenate([jnp.concatenate([obs_ref[k], left], 1), under, over], 0)
        image = stencil(once, coefs) + seen
        applied = stencil(image, coefs)[own_rows, own_cols]
        image = image[own_rows, own_cols]
        image_ref[k] = image
        stack.extend(pieces(image))
        lines.append(jnp.sum(probe[own_rows, own_cols] * image, 0, keepdims=True))
        lines.append(jnp.sum(image * image, 0, keepdims=True))
        lines.append(jnp.sum(applied * applied, 0, keepdims=True))
    found = jnp.dot(jnp.concatenate(stack, 0), col_hot, preferred_element_type=F32)
    sampled = []
    for k in range(count):
        base = 3 * k * block_rows
        high, middle, low = (
            found[base + i * block_rows : base + (i + 1) * block_rows] for i in range(3)
        )
        sampled.append(jnp.sum(((low + middle) + high) * row_hot, 0, keepdims=True) * live)
    spare = -count % SUBS
    sampled = jnp.concatenate(sampled + [jnp.zeros((spare, slots), F32)], 0)
    weighted = jnp.dot(
        sampled, weight_ref[...], precision=lax.Precision.HIGHEST, preferred_element_type=F32
    )
    product = jnp.sum(sampled * weighted, 1, keepdims=True)
    total = jnp.zeros((1, LANES), F32)
    out_lane = iota((1, LANES), 1)
    for k in range(count):
        for i in range(3):
            value = jnp.sum(lines[3 * k + i], 1, keepdims=True)
            if i == 2:
                value = value + product[k : k + 1]
            total = jnp.where(out_lane == i * count + k, value, total)
    sums_ref[...] = jnp.broadcast_to(total[None], sums_ref.shape)


def finish_kernel(sums_ref, probes_ref, image_ref, solution_ref, trace_ref):
    count, block_rows, block_cols = image_ref.shape
    cells_total = float(block_rows * block_cols * sums_ref.shape[0])
    first = jnp.sum(sums_ref[...], 0)
    second = roll(first, -count, 1)
    third = roll(first, -2 * count, 1)
    step = cells_total / first
    growth = step * step * second * (1.0 / cells_total)
    ratio = growth - 1.0
    bend = step * step * step * third * (1.0 / cells_total) - growth * growth
    next_step = step * ratio / bend
    on_probe = step + next_step * growth
    on_image = step * next_step
    used = iota(first.shape, 1) < count
    trace = jnp.where(used, step + next_step * ratio, 0.0)
    trace_ref[...] = jnp.sum(trace, 1, keepdims=True) * (cells_total / count)
    for k in range(count):
        solution_ref[k] = (
            on_probe[:, k : k + 1] * probes_ref[k, :block_rows, :block_cols]
            - on_image[:, k : k + 1] * image_ref[k]
        )


def per_device(
    probe_seeds, damping, coupling_x, coupling_y, sensor_count, sensor_cells, obs_weight
):
    block_rows, block_cols = damping.shape
    count = probe_seeds.shape[0]
    slots = obs_weight.shape[-1]
    cells = sensor_cells.reshape(1, slots)
    weight = obs_weight.reshape(slots, slots)
    wide_rows, wide_cols = block_rows + 2 * SUBS, block_cols + LANES
    devices = lax.axis_size("gx") * lax.axis_size("gy")
    full = jax.ShapeDtypeStruct

    to_left, to_right = pl.pallas_call(
        side_pack_kernel,
        out_shape=[full((block_rows, LANES), F32)] * 2,
        in_specs=[VMEM] * 3,
        out_specs=[VMEM] * 2,
    )(damping, coupling_x, coupling_y)
    from_right = shifted(to_left, "gy", -1)
    from_left = shifted(to_right, "gy", 1)

    probes, observed, obs_to_left, obs_to_right = pl.pallas_call(
        observe_kernel,
        out_shape=[
            full((count, wide_rows, wide_cols), F32),
            full((count, block_rows, block_cols), F32),
            full((block_rows, LANES), F32),
            full((block_rows, LANES), F32),
        ],
        in_specs=[SMEM, SMEM, VMEM, VMEM],
        out_specs=[VMEM] * 4,
    )(probe_seeds, sensor_count, cells, weight)

    edge_rows = SUBS + count + -count % SUBS
    to_above, to_below = pl.pallas_call(
        edge_pack_kernel,
        out_shape=[full((edge_rows, wide_cols), F32)] * 2,
        in_specs=[VMEM] * 6,
        out_specs=[VMEM] * 2,
    )(damping, coupling_x, coupling_y, from_right, from_left, observed)
    from_below = shifted(to_above, "gx", -1)
    from_above = shifted(to_below, "gx", 1)
    obs_right = shifted(obs_to_left, "gy", -1)
    obs_left = shifted(obs_to_right, "gy", 1)

    image, sums = pl.pallas_call(
        image_kernel,
        out_shape=[full((count, block_rows, block_cols), F32), full((devices, 1, LANES), F32)],
        in_specs=[SMEM] + [VMEM] * 13,
        out_specs=[VMEM] * 2,
        scratch_shapes=[pltpu.VMEM((wide_rows, wide_cols), F32)] * 5,
    )(
        sensor_count,
        cells,
        weight,
        damping,
        coupling_x,
        coupling_y,
        from_right,
        from_left,
        from_below,
        from_above,
        observed,
        obs_right,
        obs_left,
        probes,
    )
    sums = lax.all_to_all(sums, ("gx", "gy"), 0, 0, tiled=True)
    solved, trace = pl.pallas_call(
        finish_kernel,
        out_shape=[full((count, block_rows, block_cols), F32), full((1, 1), F32)],
        in_specs=[VMEM] * 3,
        out_specs=[VMEM] * 2,
    )(sums, probes, image)
    return solved, trace[0, 0]


def solution(mesh):
    placed = (
        P(),
        P("gx", "gy"),
        P("gx", "gy"),
        P("gx", "gy"),
        P("gx", "gy"),
        P("gx", "gy", None),
        P("gx", "gy", None, None),
    )
    return jax.shard_map(
        per_device,
        mesh=mesh,
        in_specs=placed,
        out_specs=(P(None, "gx", "gy"), P()),
        check_vma=False,
    )
```

time: 212 us -> 39.8 us (0.19)
  blocking collectives: 116 us -> 10.2 us
  local copies, waits for them, and re-layouts: 31 us -> 1.2 us
  other arithmetic: 16.5 us -> 0 us
  starting transfers between devices: 24.2 us -> 8.71 us
  waiting for transfers between devices: 19.3 us -> 6.71 us
  Pallas kernels: 0 us -> 11.3 us
    psum x3 -> x0, blocking collectives: 116 us -> none  [the longest x1 41.2 us: per_device(): total = lax.psum(jnp.sum(probes * solution), ('gx', 'gy'))]
    ppermute x16 -> x0, starting transfers between devices: 24.2 us -> none  [the longest x8 19.9 us: with_halo(): lax.ppermute(head, axis, [((i + 1) % count, i) for i in range(count)])]
    ppermute x16 -> x0, waiting for transfers between devices: 19.3 us -> none  [the longest x8 15.5 us: with_halo(): lax.ppermute(tail, axis, [(i, (i + 1) % count) for i in range(count)])]
    pallas_call x0 -> x5, Pallas kernels: none -> 11.3 us  [the longest x1 3.35 us: per_device(): pl.pallas_call(image_kernel, out_shape=[full((count, block_rows, block_co...]
    reshape x2 -> x0, local copies, waits for them, and re-layouts: 10.5 us -> none  [observe(): jnp.zeros_like(flat).at[:, cell_ids].add(weighted).reshape(field.shape)]
    scatter-add x2 -> x0, other arithmetic: 10.3 us -> none  [observe(): jnp.zeros_like(flat).at[:, cell_ids].add(weighted).reshape(field.shape)]
    all_to_all x0 -> x1, blocking collectives: none -> 10.2 us  [per_device(): sums = lax.all_to_all(sums, ('gx', 'gy'), 0, 0, tiled=True)]
    ppermute x2 -> x6, starting transfers between devices: 0.01 us -> 8.71 us  [shifted(): return lax.ppermute(value, axis, pairs)]
  transfers between devices with their start and end apart: 18 -> 6, of which waited for: 8 -> 2; matrix products, arithmetic and copies ran while one was open for 20% -> 0% of each run, Pallas kernels for 0% -> 11%
where the time goes in v1:
time: 39.8 us; the launch traced here: 39.5 us
  Pallas kernels  11.3 us (28%)
  blocking collectives  10.2 us (26%)
  starting transfers between devices  8.71 us (22%)
  waiting for transfers between devices  6.71 us (17%)
  between operations  1.33 us (3%)
  local copies, waits for them, and re-layouts  1.2 us (3%)
    all_to_all x1, blocking collectives, per_device(): sums = lax.all_to_all(sums, ('gx', 'gy'), 0, 0, tiled=True)  10.2 us
    ppermute x6, starting transfers between devices, shifted(): return lax.ppermute(value, axis, pairs)  8.71 us
    ppermute x6, waiting for transfers between devices, shifted(): return lax.ppermute(value, axis, pairs)  6.71 us
    pallas_call x1, Pallas kernels, per_device(): pl.pallas_call(image_kernel, out_shape=[full((count, block_rows, block_co...  3.35 us
    pallas_call x1, Pallas kernels, per_device(): pl.pallas_call(observe_kernel, out_shape=[full((count, wide_rows, wide_co...  2.48 us
    pallas_call x1, Pallas kernels, per_device(): pl.pallas_call(finish_kernel, out_shape=[full((count, block_rows, block_c...  2.06 us
    pallas_call x1, Pallas kernels, per_device(): pl.pallas_call(edge_pack_kernel, out_shape=[full((edge_rows, wide_cols),...  1.79 us
    pallas_call x1, Pallas kernels, per_device(): pl.pallas_call(side_pack_kernel, out_shape=[full((block_rows, LANES), F32...  1.62 us
  transfers between devices with their start and end apart: 6, of which 2 were waited for; matrix products, arithmetic and copies ran while one was open for 0% of the time, Pallas kernels for 11%

profile of v1, /device:TPU:0, one launch (start us, length us, event | category | flops | bytes accessed | tf_op | source)
XLA Modules:
  0.0 39.5 jit_solution(14772575620228204221)
XLA Ops:
  0.6 1.6 %shard_map.86 = (f32[64,128]{1,0:T(8,128)}, f32[64,128]{1,0:T(8,128)}) custom-call(f32[64,256]{1,0:T(8,128)} %d_ref.5, f32[64,256]{1,0:T(8,128)} %cx_ref.5, f32[64,256]{1,0:T(8,128)} %cy_ref.5), custom_call_target="tpu_custom_call" | custom-call | tf_op jit(solution)/shard_map/pallas_call | solution.py:316
  2.2 2.4 %collective-permute-start = (f32[64,128]{1,0:T(8,128)}, f32[64,128]{1,0:T(8,128)S(1)}, u32[]{:S(2)}, u32[]{:S(2)}) collective-permute-start(f32[64,128]{1,0:T(8,128)} %get-tuple-element.14), channel_id=1, source_target_pairs={{0,3},{1,0},{2,1},{3,2},{4,7},{5,4},{6,5},{7,6},{8,11},{9,8},{10,9... | collective-permute-start | bytes 98312 | tf_op jit(solution)/shard_map/ppermute | solution.py:19
  4.7 0.0 collective-permute-start.1
  5.3 2.5 %shard_map.87 = (f32[4,80,384]{2,1,0:T(8,128)}, f32[4,64,256]{2,1,0:T(8,128)}, f32[64,128]{1,0:T(8,128)}, f32[64,128]{1,0:T(8,128)}) custom-call(s32[4]{0:T(128)} %seeds_ref.1, s32[1,1]{1,0:T(1,128)S(6)} %copy.9.count_ref, s32[1,256]{1,0:T(1,128)} %bitcast.5, f32[256,256]{1,0:T(8,128)} %bitcast.3), custom_call_target="tpu_custom_call" | custom-call | tf_op jit(solution)/shard_map/pallas_call | solution.py:325
  7.8 1.7 %collective-permute-start.4 = (f32[64,128]{1,0:T(8,128)}, f32[64,128]{1,0:T(8,128)S(1)}, u32[]{:S(2)}, u32[]{:S(2)}) collective-permute-start(f32[64,128]{1,0:T(8,128)} %get-tuple-element.19), channel_id=1, source_target_pairs={{0,3},{1,0},{2,1},{3,2},{4,7},{5,4},{6,5},{7,6},{8,11},{9,8},{10,9... | collective-permute-start | bytes 98312 | tf_op jit(solution)/shard_map/ppermute | solution.py:19
  9.6 0.0 collective-permute-start.5
  9.6 0.0 collective-permute-done.from_right_ref
  9.6 0.0 collective-permute-done.1.from_left_ref
  9.6 0.0 copy-start.1
  9.6 0.6 %copy-done = f32[64,128]{1,0:T(8,128)} copy-done((f32[64,128]{1,0:T(8,128)}, f32[64,128]{1,0:T(8,128)S(1)}, u32[]{:S(2)}) %copy-start) | copy-done | bytes 32792
  10.2 0.0 copy-done.1
  10.2 1.8 %shard_map.88 = (f32[16,384]{1,0:T(8,128)}, f32[16,384]{1,0:T(8,128)}) custom-call(f32[64,256]{1,0:T(8,128)} %d_ref.5, f32[64,256]{1,0:T(8,128)} %cx_ref.5, f32[64,256]{1,0:T(8,128)} %cy_ref.5, f32[64,128]{1,0:T(8,128)} %copy-done, f32[64,128]{1,0:T(8,128)} %copy-done.1, f32[4,64,256]{2,1,0:T(8,128)} %get-tuple-element.16.obs_ref), custom_call_target="tpu_custom_call" | custom-call | tf_op jit(solution)/shard_map/pallas_call | solution.py:338
  12.0 4.5 %collective-permute-start.2 = (f32[16,384]{1,0:T(8,128)}, f32[16,384]{1,0:T(8,128)S(1)}, u32[]{:S(2)}, u32[]{:S(2)}) collective-permute-start(f32[16,384]{1,0:T(8,128)} %get-tuple-element.17), channel_id=1, source_target_pairs={{0,28},{4,0},{8,4},{12,8},{16,12},{20,16},{24,20},{28,24},{1,29},{... | collective-permute-start | bytes 73736 | tf_op jit(solution)/shard_map/ppermute | solution.py:19
  16.5 0.0 collective-permute-start.3
  16.5 0.0 collective-permute-done.4.obs_right_ref
  16.5 0.0 collective-permute-done.5.obs_left_ref
  16.5 0.0 copy-start.3
  16.5 1.7 %collective-permute-done.2.from_below_ref = f32[16,384]{1,0:T(8,128)S(1)} collective-permute-done((f32[16,384]{1,0:T(8,128)}, f32[16,384]{1,0:T(8,128)S(1)}, u32[]{:S(2)}, u32[]{:S(2)}) %collective-permute-start.2) | collective-permute-done | bytes 24608 | tf_op jit(solution)/shard_map/ppermute | solution.py:19
  18.2 5.0 %collective-permute-done.3.from_above_ref = f32[16,384]{1,0:T(8,128)S(1)} collective-permute-done((f32[16,384]{1,0:T(8,128)}, f32[16,384]{1,0:T(8,128)S(1)}, u32[]{:S(2)}, u32[]{:S(2)}) %collective-permute-start.3) | collective-permute-done | bytes 24608 | tf_op jit(solution)/shard_map/ppermute | solution.py:19
  23.3 0.0 copy-done.4
  23.3 0.6 %copy-done.5 = f32[16,384]{1,0:T(8,128)} copy-done((f32[16,384]{1,0:T(8,128)}, f32[16,384]{1,0:T(8,128)S(1)}, u32[]{:S(2)}) %copy-start.5) | copy-done | bytes 24600
  23.8 3.4 %shard_map.89 = (f32[4,64,256]{2,1,0:T(8,128)}, f32[32,1,128]{2,1,0:T(1,128)}) custom-call(s32[1,1]{1,0:T(1,128)S(6)} %copy.9.count_ref, s32[1,256]{1,0:T(1,128)} %bitcast.6, f32[256,256]{1,0:T(8,128)} %bitcast.4, f32[64,256]{1,0:T(8,128)} %d_ref.5, f32[64,256]{1,0:T(8,128)} %cx_ref.5, f32[64,256]{1,0:T(8,128)} %cy_ref.5, f32[64,128]{1,0:T(8,128)} %copy-done, ...), custom_call_target="tpu_custom_call" | custom-call | tf_op jit(solution)/shard_map/pallas_call | solution.py:349
  27.2 10.2 %all_to_all.5.sums_ref = f32[32,1,128]{2,1,0:T(1,128)} all-to-all(f32[32,1,128]{2,1,0:T(1,128)} %get-tuple-element.22), channel_id=1, replica_groups=mesh['gx'=8,'gy'=4] {'gx','gy'}, dimensions={0} | all-to-all | bytes 32768 | tf_op jit(solution)/shard_map/all_to_all | solution.py:371
  37.4 2.1 %shard_map.90 = (f32[4,64,256]{2,1,0:T(8,128)}, f32[1,1]{1,0:T(1,128)}) custom-call(f32[32,1,128]{2,1,0:T(1,128)} %all_to_all.5.sums_ref, f32[4,80,384]{2,1,0:T(8,128)} %get-tuple-element.21.probes_ref, f32[4,64,256]{2,1,0:T(8,128)} %get-tuple-element.23.image_ref), custom_call_target="tpu_custom_call" | custom-call | tf_op jit(solution)/shard_map/pallas_call | solution.py:372
  (6 shorter events, 0.0 us)
Async XLA Ops:
  2.2 7.3 %collective-permute-start = (f32[64,128]{1,0:T(8,128)}, f32[64,128]{1,0:T(8,128)S(1)}, u32[]{:S(2)}, u32[]{:S(2)}) collective-permute-start(f32[64,128]{1,0:T(8,128)} %get-tuple-element.14), channel_id=1, source_target_pairs={{0,3},{1,0},{2,1},{3,2},{4,7},{5,4},{6,5},{7,6},{8,11},{9,8},{10,9... | collective-permute-start | bytes 98312 | tf_op jit(solution)/shard_map/ppermute | solution.py:19
  4.7 4.9 %collective-permute-start.1 = (f32[64,128]{1,0:T(8,128)}, f32[64,128]{1,0:T(8,128)S(1)}, u32[]{:S(2)}, u32[]{:S(2)}) collective-permute-start(f32[64,128]{1,0:T(8,128)} %get-tuple-element.15), channel_id=1, source_target_pairs={{0,1},{1,2},{2,3},{3,0},{4,5},{5,6},{6,7},{7,4},{8,9},{9,10},{10,1... | collective-permute-start | bytes 98312 | tf_op jit(solution)/shard_map/ppermute | solution.py:19
  7.8 8.7 %collective-permute-start.4 = (f32[64,128]{1,0:T(8,128)}, f32[64,128]{1,0:T(8,128)S(1)}, u32[]{:S(2)}, u32[]{:S(2)}) collective-permute-start(f32[64,128]{1,0:T(8,128)} %get-tuple-element.19), channel_id=1, source_target_pairs={{0,3},{1,0},{2,1},{3,2},{4,7},{5,4},{6,5},{7,6},{8,11},{9,8},{10,9... | collective-permute-start | bytes 98312 | tf_op jit(solution)/shard_map/ppermute | solution.py:19
  9.6 7.0 %collective-permute-start.5 = (f32[64,128]{1,0:T(8,128)}, f32[64,128]{1,0:T(8,128)S(1)}, u32[]{:S(2)}, u32[]{:S(2)}) collective-permute-start(f32[64,128]{1,0:T(8,128)} %get-tuple-element.20), channel_id=1, source_target_pairs={{0,1},{1,2},{2,3},{3,0},{4,5},{5,6},{6,7},{7,4},{8,9},{9,10},{10,1... | collective-permute-start | bytes 98312 | tf_op jit(solution)/shard_map/ppermute | solution.py:19
  9.6 0.6 %copy-start = (f32[64,128]{1,0:T(8,128)}, f32[64,128]{1,0:T(8,128)S(1)}, u32[]{:S(2)}) copy-start(f32[64,128]{1,0:T(8,128)S(1)} %collective-permute-done.from_right_ref) | copy-start | bytes 98308
  9.6 0.6 %copy-start.1 = (f32[64,128]{1,0:T(8,128)}, f32[64,128]{1,0:T(8,128)S(1)}, u32[]{:S(2)}) copy-start(f32[64,128]{1,0:T(8,128)S(1)} %collective-permute-done.1.from_left_ref) | copy-start | bytes 98308
  12.0 6.3 %collective-permute-start.2 = (f32[16,384]{1,0:T(8,128)}, f32[16,384]{1,0:T(8,128)S(1)}, u32[]{:S(2)}, u32[]{:S(2)}) collective-permute-start(f32[16,384]{1,0:T(8,128)} %get-tuple-element.17), channel_id=1, source_target_pairs={{0,28},{4,0},{8,4},{12,8},{16,12},{20,16},{24,20},{28,24},{1,29},{... | collective-permute-start | bytes 73736 | tf_op jit(solution)/shard_map/ppermute | solution.py:19
  16.5 6.7 %collective-permute-start.3 = (f32[16,384]{1,0:T(8,128)}, f32[16,384]{1,0:T(8,128)S(1)}, u32[]{:S(2)}, u32[]{:S(2)}) collective-permute-start(f32[16,384]{1,0:T(8,128)} %get-tuple-element.18), channel_id=1, source_target_pairs={{0,4},{4,8},{8,12},{12,16},{16,20},{20,24},{24,28},{28,0},{1,5},{5... | collective-permute-start | bytes 73736 | tf_op jit(solution)/shard_map/ppermute | solution.py:19
  16.5 6.7 %copy-start.2 = (f32[64,128]{1,0:T(8,128)}, f32[64,128]{1,0:T(8,128)S(1)}, u32[]{:S(2)}) copy-start(f32[64,128]{1,0:T(8,128)S(1)} %collective-permute-done.4.obs_right_ref) | copy-start | bytes 98308
  16.5 6.7 %copy-start.3 = (f32[64,128]{1,0:T(8,128)}, f32[64,128]{1,0:T(8,128)S(1)}, u32[]{:S(2)}) copy-start(f32[64,128]{1,0:T(8,128)S(1)} %collective-permute-done.5.obs_left_ref) | copy-start | bytes 98308
  18.2 5.0 %copy-start.4 = (f32[16,384]{1,0:T(8,128)}, f32[16,384]{1,0:T(8,128)S(1)}, u32[]{:S(2)}) copy-start(f32[16,384]{1,0:T(8,128)S(1)} %collective-permute-done.2.from_below_ref) | copy-start | bytes 73732
  23.3 0.6 %copy-start.5 = (f32[16,384]{1,0:T(8,128)}, f32[16,384]{1,0:T(8,128)S(1)}, u32[]{:S(2)}) copy-start(f32[16,384]{1,0:T(8,128)S(1)} %collective-permute-done.3.from_above_ref) | copy-start | bytes 73732

commit v2 on v1

--- a/solution.py
+++ b/solution.py
@@ -9,14 +9,18 @@
 SUBS = 8
 F32 = jnp.float32
 BF16 = jnp.bfloat16
+SMEM = pl.BlockSpec(memory_space=pltpu.SMEM)
 VMEM = pl.BlockSpec(memory_space=pltpu.VMEM)
-SMEM = pl.BlockSpec(memory_space=pltpu.SMEM)
 
 
 def shifted(value, axis, steps):
     count = lax.axis_size(axis)
     pairs = [(source, (source + steps) % count) for source in range(count)]
     return lax.ppermute(value, axis, pairs)
+
+
+def on_chip(*values):
+    return tuple(pltpu.with_memory_space_constraint(value, pltpu.VMEM) for value in values)
 
 
 def sign_bits(seeds, row_ids, col_ids):
@@ -56,21 +60,28 @@
     return row_hot, col_hot
 
 
-def side_pack_kernel(d_ref, cx_ref, cy_ref, left_ref, right_ref):
-    block_rows, block_cols = d_ref.shape
+def load_kernel(
+    seeds_in, cells_in, weight_in, d_in, cx_in, cy_in,
+    seeds_ref, cells_ref, weight_ref, d_ref, cx_ref, cy_ref, left_ref, right_ref,
+):
+    block_rows, block_cols = d_in.shape
+    d, cx, cy = d_in[...], cx_in[...], cy_in[...]
+    d_ref[...], cx_ref[...], cy_ref[...] = d, cx, cy
     lane = iota((block_rows, LANES), 1)
-    first = slice(0, LANES)
-    last = slice(block_cols - LANES, block_cols)
     left_ref[...] = jnp.where(
         lane < 3,
-        cy_ref[:, first],
-        jnp.where(lane < 6, roll(d_ref[:, first], 3, 1), roll(cx_ref[:, first], 6, 1)),
-    )
+        cy[:, :LANES],
+        jnp.where(lane < 6, roll(d[:, :LANES], 3, 1), roll(cx[:, :LANES], 6, 1)),
+    )
+    last = slice(block_cols - LANES, block_cols)
     right_ref[...] = jnp.where(
         lane >= LANES - 3,
-        cy_ref[:, last],
-        jnp.where(lane >= LANES - 6, roll(d_ref[:, last], -3, 1), roll(cx_ref[:, last], -6, 1)),
-    )
+        cy[:, last],
+        jnp.where(lane >= LANES - 6, roll(d[:, last], -3, 1), roll(cx[:, last], -6, 1)),
+    )
+    seeds_ref[...] = seeds_in[...]
+    cells_ref[...] = cells_in[...]
+    weight_ref[...] = weight_in[...]
 
 
 def side_tiles(from_right, from_left):
@@ -82,7 +93,7 @@
 
 
 def observe_kernel(
-    seeds_ref, count_ref, cells_ref, weight_ref, probes_ref, obs_ref, left_ref, right_ref
+    number_ref, seeds_ref, cells_ref, weight_ref, probes_ref, obs_ref, live_ref
 ):
     count, wide_rows, wide_cols = probes_ref.shape
     _, block_rows, block_cols = obs_ref.shape
@@ -98,8 +109,9 @@
     which = iota((padded, slots), 0)
     seeds = jnp.zeros((padded, slots), jnp.int32)
     for k in range(count):
-        seeds = jnp.where(which == k, seeds_ref[k], seeds)
-    live = jnp.where(iota((1, slots), 1) < count_ref[0, 0], 1.0, 0.0)
+        seeds = jnp.where(which == k, seeds_ref[:, k : k + 1], seeds)
+    live = jnp.where(iota((1, slots), 1) < number_ref[0, 0], 1.0, 0.0)
+    live_ref[...] = live
     sampled = sign_bits(seeds, rows + row_start, cols + col_start) * live
     weighted = (
         jnp.dot(sampled, weight_ref[...], precision=lax.Precision.HIGHEST, preferred_element_type=F32)
@@ -113,22 +125,12 @@
     spread = lax.dot_general(
         jnp.concatenate(stack, 0), col_hot, (((1,), (1,)), ((), ())), preferred_element_type=F32
     )
-    lane = iota((block_rows, LANES), 1)
-    left = jnp.zeros((block_rows, LANES), F32)
-    right = jnp.zeros((block_rows, LANES), F32)
     for k in range(count):
         base = 3 * k * block_rows
         high, middle, low = (
             spread[base + i * block_rows : base + (i + 1) * block_rows] for i in range(3)
         )
-        total = (low + middle) + high
-        obs_ref[k] = total
-        left = jnp.where(lane == k, roll(total[:, :LANES], k, 1), left)
-        right = jnp.where(
-            lane == LANES - count + k, roll(total[:, block_cols - LANES :], k + 1 - count, 1), right
-        )
-    left_ref[...] = left
-    right_ref[...] = right
+        obs_ref[k] = (low + middle) + high
 
     wide = (wide_rows, wide_cols)
     row_ids = iota(wide, 0)
@@ -140,11 +142,12 @@
     col_ids = jnp.where(col_ids < 0, col_ids + cols_total, col_ids)
     col_ids = jnp.where(col_ids >= cols_total, col_ids - cols_total, col_ids)
     for k in range(count):
-        probes_ref[k] = sign_bits(seeds_ref[k], row_ids, col_ids)
+        probes_ref[k] = sign_bits(seeds_ref[:, k : k + 1], row_ids, col_ids)
 
 
 def edge_pack_kernel(
-    d_ref, cx_ref, cy_ref, from_right_ref, from_left_ref, obs_ref, up_ref, down_ref
+    d_ref, cx_ref, cy_ref, from_right_ref, from_left_ref, obs_ref,
+    up_ref, down_ref, left_ref, right_ref,
 ):
     count, block_rows, block_cols = obs_ref.shape
     wide_cols = block_cols + LANES
@@ -173,6 +176,15 @@
         sub >= SUBS - 3, cx, jnp.where(sub >= SUBS - 5, roll(d, -3, 0), roll(cy, -5, 0))
     )
     down_ref[SUBS:] = observed(block_rows - 1)
+    lane = iota((block_rows, LANES), 1)
+    left = jnp.zeros((block_rows, LANES), F32)
+    right = jnp.zeros((block_rows, LANES), F32)
+    for k in range(count):
+        left = jnp.where(lane == k, roll(obs_ref[k, :, :LANES], k, 1), left)
+        last = obs_ref[k, :, block_cols - LANES :]
+        right = jnp.where(lane == LANES - count + k, roll(last, k + 1 - count, 1), right)
+    left_ref[...] = left
+    right_ref[...] = right
 
 
 def stencil(v, coefs):
@@ -187,7 +199,7 @@
 
 
 def image_kernel(
-    count_ref,
+    live_ref,
     cells_ref,
     weight_ref,
     d_ref,
@@ -233,7 +245,7 @@
 
     slots = cells_ref.shape[1]
     row_hot, col_hot = one_hots(cells_ref[...], block_rows, block_cols)
-    live = jnp.where(iota((1, slots), 1) < count_ref[0, 0], 1.0, 0.0)
+    live = live_ref[...]
     lane = iota((block_rows, LANES), 1)
     sub = iota((SUBS, block_cols + LANES), 0)
     stack, lines = [], []
@@ -307,74 +319,90 @@
     block_rows, block_cols = damping.shape
     count = probe_seeds.shape[0]
     slots = obs_weight.shape[-1]
-    cells = sensor_cells.reshape(1, slots)
-    weight = obs_weight.reshape(slots, slots)
     wide_rows, wide_cols = block_rows + 2 * SUBS, block_cols + LANES
     devices = lax.axis_size("gx") * lax.axis_size("gy")
+    edge_rows = SUBS + count + -count % SUBS
     full = jax.ShapeDtypeStruct
 
-    to_left, to_right = pl.pallas_call(
-        side_pack_kernel,
-        out_shape=[full((block_rows, LANES), F32)] * 2,
-        in_specs=[VMEM] * 3,
-        out_specs=[VMEM] * 2,
-    )(damping, coupling_x, coupling_y)
+    def call(kernel, args, outs, scratch=(), scalars=0):
+        return pl.pallas_call(
+            kernel,
+            out_shape=outs,
+            in_specs=[SMEM] * scalars + [VMEM] * (len(args) - scalars),
+            out_specs=[VMEM] * len(outs),
+            scratch_shapes=scratch,
+        )(*args)
+
+    block = pltpu.VMEM((block_rows, block_cols), F32)
+    blocks = pltpu.VMEM((count, block_rows, block_cols), F32)
+    wide_blocks = pltpu.VMEM((count, wide_rows, wide_cols), F32)
+    column = pltpu.VMEM((block_rows, LANES), F32)
+    rows = pltpu.VMEM((edge_rows, wide_cols), F32)
+
+    seeds, cells, weight, *coefs, to_left, to_right = call(
+        load_kernel,
+        (
+            probe_seeds.reshape(1, count),
+            sensor_cells.reshape(1, slots),
+            obs_weight.reshape(slots, slots),
+            damping,
+            coupling_x,
+            coupling_y,
+        ),
+        [
+            pltpu.VMEM((1, count), jnp.int32),
+            pltpu.VMEM((1, slots), jnp.int32),
+            pltpu.VMEM((slots, slots), F32),
+            block,
+            block,
+            block,
+            column,
+            column,
+        ],
+    )
+    seeds, cells, weight, *coefs = on_chip(seeds, cells, weight, *coefs)
     from_right = shifted(to_left, "gy", -1)
     from_left = shifted(to_right, "gy", 1)
-
-    probes, observed, obs_to_left, obs_to_right = pl.pallas_call(
-        observe_kernel,
-        out_shape=[
-            full((count, wide_rows, wide_cols), F32),
-            full((count, block_rows, block_cols), F32),
-            full((block_rows, LANES), F32),
-            full((block_rows, LANES), F32),
-        ],
-        in_specs=[SMEM, SMEM, VMEM, VMEM],
-        out_specs=[VMEM] * 4,
-    )(probe_seeds, sensor_count, cells, weight)
-
-    edge_rows = SUBS + count + -count % SUBS
-    to_above, to_below = pl.pallas_call(
-        edge_pack_kernel,
-        out_shape=[full((edge_rows, wide_cols), F32)] * 2,
-        in_specs=[VMEM] * 6,
-        out_specs=[VMEM] * 2,
-    )(damping, coupling_x, coupling_y, from_right, from_left, observed)
+    sides = on_chip(from_right, from_left)
+
+    probes, observed, live = on_chip(
+        *call(
+            observe_kernel,
+            (sensor_count, seeds, cells, weight),
+            [wide_blocks, blocks, pltpu.VMEM((1, slots), F32)],
+            scalars=1,
+        )
+    )
+    to_above, to_below, obs_to_left, obs_to_right = call(
+        edge_pack_kernel, (*coefs, *sides, observed), [rows, rows, column, column]
+    )
     from_below = shifted(to_above, "gx", -1)
     from_above = shifted(to_below, "gx", 1)
     obs_right = shifted(obs_to_left, "gy", -1)
     obs_left = shifted(obs_to_right, "gy", 1)
 
-    image, sums = pl.pallas_call(
+    image, sums = call(
         image_kernel,
-        out_shape=[full((count, block_rows, block_cols), F32), full((devices, 1, LANES), F32)],
-        in_specs=[SMEM] + [VMEM] * 13,
-        out_specs=[VMEM] * 2,
-        scratch_shapes=[pltpu.VMEM((wide_rows, wide_cols), F32)] * 5,
-    )(
-        sensor_count,
-        cells,
-        weight,
-        damping,
-        coupling_x,
-        coupling_y,
-        from_right,
-        from_left,
-        from_below,
-        from_above,
-        observed,
-        obs_right,
-        obs_left,
-        probes,
+        (
+            live,
+            cells,
+            weight,
+            *coefs,
+            *sides,
+            *on_chip(from_below, from_above),
+            observed,
+            *on_chip(obs_right, obs_left),
+            probes,
+        ),
+        [blocks, pltpu.VMEM((devices, 1, LANES), F32)],
+        [pltpu.VMEM((wide_rows, wide_cols), F32)] * 5,
     )
     sums = lax.all_to_all(sums, ("gx", "gy"), 0, 0, tiled=True)
-    solved, trace = pl.pallas_call(
+    solved, trace = call(
         finish_kernel,
-        out_shape=[full((count, block_rows, block_cols), F32), full((1, 1), F32)],
-        in_specs=[VMEM] * 3,
-        out_specs=[VMEM] * 2,
-    )(sums, probes, image)
+        (*on_chip(sums), probes, *on_chip(image)),
+        [full((count, block_rows, block_cols), F32), full((1, 1), F32)],
+    )
     return solved, trace[0, 0]
 
 

time: 39.8 us -> 30.9 us (0.78)
  Pallas kernels: 11.3 us -> 4.5 us
  waiting for transfers between devices: 6.71 us -> 8.4 us
  blocking collectives: 10.2 us -> 8.87 us
  local copies, waits for them, and re-layouts: 1.2 us -> 0 us
  starting transfers between devices: 8.71 us -> 7.67 us
    pallas_call x5, Pallas kernels: 11.3 us -> 4.5 us  [call(): pl.pallas_call(kernel, out_shape=outs, in_specs=[SMEM] * scalars + [VMEM]...]
    ppermute x6, waiting for transfers between devices: 6.71 us -> 8.4 us  [shifted(): return lax.ppermute(value, axis, pairs)]
    all_to_all x1, blocking collectives: 10.2 us -> 8.87 us  [per_device(): sums = lax.all_to_all(sums, ('gx', 'gy'), 0, 0, tiled=True)]
    unnamed x12 -> x0, local copies, waits for them, and re-layouts: 1.2 us -> none
    ppermute x6, starting transfers between devices: 8.71 us -> 7.67 us  [shifted(): return lax.ppermute(value, axis, pairs)]
  transfers between devices with their start and end apart: 6 -> 6, of which waited for: 2 -> 4; matrix products, arithmetic and copies ran while one was open for 0% -> 0% of each run, Pallas kernels for 11% -> 3%
where the time goes in v2:
time: 30.9 us; the launch traced here: 30.8 us
  blocking collectives  8.87 us (29%)
  waiting for transfers between devices  8.4 us (27%)
  starting transfers between devices  7.67 us (25%)
  Pallas kernels  4.5 us (15%)
  between operations  1.32 us (4%)
    all_to_all x1, blocking collectives, per_device(): sums = lax.all_to_all(sums, ('gx', 'gy'), 0, 0, tiled=True)  8.87 us
    ppermute x6, waiting for transfers between devices, shifted(): return lax.ppermute(value, axis, pairs)  8.4 us
    ppermute x6, starting transfers between devices, shifted(): return lax.ppermute(value, axis, pairs)  7.67 us
    pallas_call x5, Pallas kernels, call(): pl.pallas_call(kernel, out_shape=outs, in_specs=[SMEM] * scalars + [VMEM]...  4.5 us
  transfers between devices with their start and end apart: 6, of which 4 were waited for; matrix products, arithmetic and copies ran while one was open for 0% of the time, Pallas kernels for 3%

profile of v2, /device:TPU:0, one launch (start us, length us, event | category | flops | bytes accessed | tf_op | source)
XLA Modules:
  0.0 30.8 jit_solution(6946221794918768628)
XLA Ops:
  0.6 1.1 %shard_map.86 = (s32[1,4]{1,0:T(1,128)S(1)}, s32[1,256]{1,0:T(1,128)S(1)}, f32[256,256]{1,0:T(8,128)S(1)}, f32[64,256]{1,0:T(8,128)S(1)}, f32[64,256]{1,0:T(8,12...) custom-call(s32[1,4]{1,0:T(1,128)} %bitcast.6, s32[1,256]{1,0:T(1,128)} %bitcast.5, ...), custom_call_target="tpu_custom_call" | custom-call | tf_op jit(solution)/shard_map/pallas_call | solution.py:328
  1.8 2.5 %collective-permute-start = (f32[64,128]{1,0:T(8,128)S(1)}, f32[64,128]{1,0:T(8,128)S(1)}, u32[]{:S(2)}, u32[]{:S(2)}) collective-permute-start(f32[64,128]{1,0:T(8,128)S(1)} %get-tuple-element.28), channel_id=1, source_target_pairs={{0,3},{1,0},{2,1},{3,2},{4,7},{5,4},{6,5},{7,6},{8,11},{9,8},{10,9... | collective-permute-start | bytes 98312 | tf_op jit(solution)/shard_map/ppermute | solution.py:19
  4.3 0.0 collective-permute-start.1
  4.9 0.8 %shard_map.87 = (f32[4,80,384]{2,1,0:T(8,128)S(1)}, f32[4,64,256]{2,1,0:T(8,128)S(1)}, f32[1,256]{1,0:T(1,128)S(1)}) custom-call(s32[1,1]{1,0:T(1,128)S(6)} %copy.9.number_ref, s32[1,4]{1,0:T(1,128)S(1)} %get-tuple-element.21.seeds_ref, s32[1,256]{1,0:T(1,128)S(1)} %get-tuple-element.22.cells_ref, f32[256,256]{1,0:T(8,128)S(1)} %get-tuple-element.23.weight_ref), custom_call_target="tpu_custom_call" | custom-call | tf_op jit(solution)/shard_map/pallas_call | solution.py:328
  5.7 0.3 collective-permute-done.from_right_ref
  6.0 1.6 %collective-permute-done.1.from_left_ref = f32[64,128]{1,0:T(8,128)S(1)} collective-permute-done((f32[64,128]{1,0:T(8,128)S(1)}, f32[64,128]{1,0:T(8,128)S(1)}, u32[]{:S(2)}, u32[]{:S(2)}) %collective-permute-start.1) | collective-permute-done | bytes 32800 | tf_op jit(solution)/shard_map/ppermute | solution.py:19
  7.6 0.1 shard_map.88
  7.7 0.6 %collective-permute-start.4 = (f32[64,128]{1,0:T(8,128)S(1)}, f32[64,128]{1,0:T(8,128)S(1)}, u32[]{:S(2)}, u32[]{:S(2)}) collective-permute-start(f32[64,128]{1,0:T(8,128)S(1)} %get-tuple-element.33), channel_id=1, source_target_pairs={{0,3},{1,0},{2,1},{3,2},{4,7},{5,4},{6,5},{7,6},{8,11},{9,8},{10,9... | collective-permute-start | bytes 98312 | tf_op jit(solution)/shard_map/ppermute | solution.py:19
  8.4 0.0 collective-permute-start.5
  8.4 4.5 %collective-permute-start.2 = (f32[16,384]{1,0:T(8,128)S(1)}, f32[16,384]{1,0:T(8,128)S(1)}, u32[]{:S(2)}, u32[]{:S(2)}) collective-permute-start(f32[16,384]{1,0:T(8,128)S(1)} %get-tuple-element.31), channel_id=1, source_target_pairs={{0,28},{4,0},{8,4},{12,8},{16,12},{20,16},{24,20},{28,24},{1,29},{... | collective-permute-start | bytes 73736 | tf_op jit(solution)/shard_map/ppermute | solution.py:19
  12.9 0.0 collective-permute-start.3
  12.9 1.5 %collective-permute-done.2.from_below_ref = f32[16,384]{1,0:T(8,128)S(1)} collective-permute-done((f32[16,384]{1,0:T(8,128)S(1)}, f32[16,384]{1,0:T(8,128)S(1)}, u32[]{:S(2)}, u32[]{:S(2)}) %collective-permute-start.2) | collective-permute-done | bytes 24608 | tf_op jit(solution)/shard_map/ppermute | solution.py:19
  14.4 5.0 %collective-permute-done.3.from_above_ref = f32[16,384]{1,0:T(8,128)S(1)} collective-permute-done((f32[16,384]{1,0:T(8,128)S(1)}, f32[16,384]{1,0:T(8,128)S(1)}, u32[]{:S(2)}, u32[]{:S(2)}) %collective-permute-start.3) | collective-permute-done | bytes 24608 | tf_op jit(solution)/shard_map/ppermute | solution.py:19
  19.4 0.0 collective-permute-done.4.obs_right_ref
  19.4 0.0 collective-permute-done.5.obs_left_ref
  19.5 1.5 %shard_map.89 = (f32[4,64,256]{2,1,0:T(8,128)S(1)}, f32[32,1,128]{2,1,0:T(1,128)S(1)}) custom-call(f32[1,256]{1,0:T(1,128)S(1)} %get-tuple-element.24.live_ref, s32[1,256]{1,0:T(1,128)S(1)} %get-tuple-element.22.cells_ref, f32[256,256]{1,0:T(8,128)S(1)} %get-tuple-element.23.weight_ref, f32[64,256]{1,0:T(8,128)S(1)} %get-tuple-element.25.d_ref, ...), custom_call_target="tpu_custom_call" | custom-call | tf_op jit(solution)/shard_map/pallas_call | solution.py:328
  20.9 8.9 %all_to_all.5.sums_ref = f32[32,1,128]{2,1,0:T(1,128)S(1)} all-to-all(f32[32,1,128]{2,1,0:T(1,128)S(1)} %get-tuple-element.36), channel_id=1, replica_groups=mesh['gx'=8,'gy'=4] {'gx','gy'}, dimensions={0} | all-to-all | bytes 32768 | tf_op jit(solution)/shard_map/all_to_all | solution.py:400
  29.8 1.0 %shard_map.90 = (f32[4,64,256]{2,1,0:T(8,128)}, f32[1,1]{1,0:T(1,128)}) custom-call(f32[32,1,128]{2,1,0:T(1,128)S(1)} %all_to_all.5.sums_ref, f32[4,80,384]{2,1,0:T(8,128)S(1)} %get-tuple-element.35.probes_ref, f32[4,64,256]{2,1,0:T(8,128)S(1)} %get-tuple-element.37.image_ref), custom_call_target="tpu_custom_call" | custom-call | tf_op jit(solution)/shard_map/pallas_call | solution.py:328
Async XLA Ops:
  1.8 4.2 %collective-permute-start = (f32[64,128]{1,0:T(8,128)S(1)}, f32[64,128]{1,0:T(8,128)S(1)}, u32[]{:S(2)}, u32[]{:S(2)}) collective-permute-start(f32[64,128]{1,0:T(8,128)S(1)} %get-tuple-element.28), channel_id=1, source_target_pairs={{0,3},{1,0},{2,1},{3,2},{4,7},{5,4},{6,5},{7,6},{8,11},{9,8},{10,9... | collective-permute-start | bytes 98312 | tf_op jit(solution)/shard_map/ppermute | solution.py:19
  4.3 3.3 %collective-permute-start.1 = (f32[64,128]{1,0:T(8,128)S(1)}, f32[64,128]{1,0:T(8,128)S(1)}, u32[]{:S(2)}, u32[]{:S(2)}) collective-permute-start(f32[64,128]{1,0:T(8,128)S(1)} %get-tuple-element.29), channel_id=1, source_target_pairs={{0,1},{1,2},{2,3},{3,0},{4,5},{5,6},{6,7},{7,4},{8,9},{9,10},{10,1... | collective-permute-start | bytes 98312 | tf_op jit(solution)/shard_map/ppermute | solution.py:19
  7.7 11.7 %collective-permute-start.4 = (f32[64,128]{1,0:T(8,128)S(1)}, f32[64,128]{1,0:T(8,128)S(1)}, u32[]{:S(2)}, u32[]{:S(2)}) collective-permute-start(f32[64,128]{1,0:T(8,128)S(1)} %get-tuple-element.33), channel_id=1, source_target_pairs={{0,3},{1,0},{2,1},{3,2},{4,7},{5,4},{6,5},{7,6},{8,11},{9,8},{10,9... | collective-permute-start | bytes 98312 | tf_op jit(solution)/shard_map/ppermute | solution.py:19
  8.4 11.1 %collective-permute-start.5 = (f32[64,128]{1,0:T(8,128)S(1)}, f32[64,128]{1,0:T(8,128)S(1)}, u32[]{:S(2)}, u32[]{:S(2)}) collective-permute-start(f32[64,128]{1,0:T(8,128)S(1)} %get-tuple-element.34), channel_id=1, source_target_pairs={{0,1},{1,2},{2,3},{3,0},{4,5},{5,6},{6,7},{7,4},{8,9},{9,10},{10,1... | collective-permute-start | bytes 98312 | tf_op jit(solution)/shard_map/ppermute | solution.py:19
  8.4 6.1 %collective-permute-start.2 = (f32[16,384]{1,0:T(8,128)S(1)}, f32[16,384]{1,0:T(8,128)S(1)}, u32[]{:S(2)}, u32[]{:S(2)}) collective-permute-start(f32[16,384]{1,0:T(8,128)S(1)} %get-tuple-element.31), channel_id=1, source_target_pairs={{0,28},{4,0},{8,4},{12,8},{16,12},{20,16},{24,20},{28,24},{1,29},{... | collective-permute-start | bytes 73736 | tf_op jit(solution)/shard_map/ppermute | solution.py:19
  12.9 6.5 %collective-permute-start.3 = (f32[16,384]{1,0:T(8,128)S(1)}, f32[16,384]{1,0:T(8,128)S(1)}, u32[]{:S(2)}, u32[]{:S(2)}) collective-permute-start(f32[16,384]{1,0:T(8,128)S(1)} %get-tuple-element.32), channel_id=1, source_target_pairs={{0,4},{4,8},{8,12},{12,16},{16,20},{20,24},{24,28},{28,0},{1,5},{5... | collective-permute-start | bytes 73736 | tf_op jit(solution)/shard_map/ppermute | solution.py:19

commit v3 on v2

v3 whole, which is shorter than its diff:
```python
import jax
import jax.numpy as jnp
from jax import lax
from jax.experimental import pallas as pl
from jax.experimental.pallas import tpu as pltpu
from jax.sharding import PartitionSpec as P


LANES = 128
SUBS = 8
F32 = jnp.float32
BF16 = jnp.bfloat16
SMEM = pl.BlockSpec(memory_space=pltpu.SMEM)
VMEM = pl.BlockSpec(memory_space=pltpu.VMEM)


def shifted(value, axis, steps):
    count = lax.axis_size(axis)
    pairs = [(source, (source + steps) % count) for source in range(count)]
    return lax.ppermute(value, axis, pairs)


def shifted_both(value):
    down, across = lax.axis_size("gx"), lax.axis_size("gy")
    pairs = [
        (x * across + y, (x + 1) % down * across + (y + 1) % across)
        for x in range(down)
        for y in range(across)
    ]
    return lax.ppermute(value, ("gx", "gy"), pairs)


def on_chip(*values):
    return tuple(pltpu.with_memory_space_constraint(value, pltpu.VMEM) for value in values)


def sign_bits(seeds, row_ids, col_ids):
    mixed = seeds * 668265261 + row_ids * 374761393 + col_ids * 1103515245
    mixed = (mixed ^ ((mixed >> 16) & 65535)) * 73244475
    mixed = (mixed ^ ((mixed >> 16) & 65535)) * 73244475
    mixed = mixed ^ ((mixed >> 16) & 65535)
    return (2 * ((mixed >> 7) & 1) - 1).astype(F32)


def iota(shape, dim):
    return lax.broadcasted_iota(jnp.int32, shape, dim)


def roll(value, steps, dim):
    return pltpu.roll(value, steps % value.shape[dim], dim)


def pieces(value):
    high = value.astype(BF16)
    rest = value - high.astype(F32)
    middle = rest.astype(BF16)
    low = (rest - middle.astype(F32)).astype(BF16)
    return high, middle, low


def split_cells(cells, block_cols):
    rows = jnp.floor((cells.astype(F32) + 0.5) * (1.0 / block_cols)).astype(jnp.int32)
    return rows, cells - rows * block_cols


def one_hots(cells, block_rows, block_cols):
    rows, cols = split_cells(cells, block_cols)
    slots = cells.shape[1]
    row_hot = jnp.where(iota((block_rows, slots), 0) == rows, 1.0, 0.0)
    col_hot = jnp.where(iota((block_cols, slots), 0) == cols, 1.0, 0.0).astype(BF16)
    return row_hot, col_hot


def compact(value, width):
    per = LANES // width
    tiles = value.shape[0] // SUBS
    lane = iota((SUBS, LANES), 1)
    packed = []
    for start in range(0, tiles, per):
        total = value[start * SUBS : (start + 1) * SUBS]
        for i in range(1, min(per, tiles - start)):
            tile = value[(start + i) * SUBS : (start + i + 1) * SUBS]
            total = jnp.where(lane < LANES - width * i, roll(tile, -width * i, 1), total)
        packed.append(total)
    return packed[0] if len(packed) == 1 else jnp.concatenate(packed, 0)


def expand(packed, rows, width):
    per = LANES // width
    tiles = []
    for i in range(rows // SUBS):
        start = i // per * SUBS
        tile = packed[start : start + SUBS]
        tiles.append(roll(tile, width * (i % per), 1) if i % per else tile)
    return jnp.concatenate(tiles, 0)


def compact_rows(rows, width):
    per = LANES // width
    return SUBS * (-(-rows // SUBS // per))


def side_width(count):
    width = 1
    while width < 13 + 3 * count:
        width *= 2
    return width


BACK_WIDTH = 8
HALO = 5


def start_kernel(
    number_ref, seeds_ref, cells_in, weight_in, d_in, cx_in, cy_in,
    cells_ref, weight_ref, d_ref, cx_ref, cy_ref, obs_ref, live_ref,
    rows_next_ref, cols_next_ref, diag_next_ref, rows_back_ref, cols_back_ref,
):
    count, block_rows, block_cols = obs_ref.shape
    row_start = lax.axis_index("gx") * block_rows
    col_start = lax.axis_index("gy") * block_cols
    slots = cells_in.shape[1]
    cells = cells_in[...]
    weight = weight_in[...]
    cells_ref[...] = cells
    weight_ref[...] = weight
    rows, cols = split_cells(cells, block_cols)
    padded = count + -count % SUBS
    which = iota((padded, slots), 0)
    seeds = jnp.zeros((padded, slots), jnp.int32)
    for k in range(count):
        seeds = jnp.where(which == k, seeds_ref[:, k : k + 1], seeds)
    live = jnp.where(iota((1, slots), 1) < number_ref[0, 0], 1.0, 0.0)
    live_ref[...] = live
    sampled = sign_bits(seeds, rows + row_start, cols + col_start) * live
    weighted = (
        jnp.dot(sampled, weight, precision=lax.Precision.HIGHEST, preferred_element_type=F32) * live
    )
    row_hot, col_hot = one_hots(cells, block_rows, block_cols)
    parts = pieces(weighted)
    stack = [
        (row_hot * part[k : k + 1].astype(F32)).astype(BF16) for k in range(count) for part in parts
    ]
    spread = lax.dot_general(
        jnp.concatenate(stack, 0), col_hot, (((1,), (1,)), ((), ())), preferred_element_type=F32
    )
    observed = []
    for k in range(count):
        base = 3 * k * block_rows
        high, middle, low = (
            spread[base + i * block_rows : base + (i + 1) * block_rows] for i in range(3)
        )
        observed.append((low + middle) + high)
        obs_ref[k] = observed[k]

    d, cx, cy = d_in[...], cx_in[...], cy_in[...]
    d_ref[...], cx_ref[...], cy_ref[...] = d, cx, cy
    tail = slice(block_rows - SUBS, block_rows)
    last = slice(block_cols - LANES, block_cols)

    sub = iota((SUBS, block_cols), 0)
    rows_next_ref[:SUBS] = cx[tail]
    rows_next_ref[SUBS : 2 * SUBS] = jnp.where(sub >= 4, d[tail], roll(cy[tail], -4, 0))
    for k in range(0, count, 2):
        tile = observed[k][tail]
        if k + 1 < count:
            tile = jnp.where(sub >= 5, tile, roll(observed[k + 1][tail], -3, 0))
        rows_next_ref[(2 + k // 2) * SUBS : (3 + k // 2) * SUBS] = tile

    lane = iota((block_rows, LANES), 1)
    side = jnp.where(lane >= LANES - 5, cy[:, last], roll(d[:, last], -5, 1))
    side = jnp.where(lane >= LANES - 9, side, roll(cx[:, last], -9, 1))
    for k in range(count):
        edge = LANES - 13 - 3 * k
        side = jnp.where(lane >= edge, side, roll(observed[k][:, last], edge, 1))
    cols_next_ref[...] = compact(side, side_width(count))

    lane = iota((SUBS, LANES), 1)
    corner = d[tail, last]
    for i, value in enumerate([cx, cy] + observed):
        edge = LANES - HALO * (i + 1)
        corner = jnp.where(lane >= edge, corner, roll(value[tail, last], edge, 1))
    diag_next_ref[...] = corner

    rows_back_ref[...] = jnp.where(
        sub == 0, cx[:SUBS], jnp.where(sub == 1, roll(d[:SUBS], 1, 0), roll(cy[:SUBS], 2, 0))
    )
    lane = iota((block_rows, LANES), 1)
    back = jnp.where(lane == LANES - 1, roll(cy[:, :LANES], -1, 1), roll(d[:, :LANES], -2, 1))
    back = jnp.where(lane >= LANES - 2, back, roll(cx[:, :LANES], -3, 1))
    cols_back_ref[...] = compact(back, BACK_WIDTH)


def probes_kernel(seeds_ref, probes_ref):
    count, wide_rows, wide_cols = probes_ref.shape
    block_rows, block_cols = wide_rows - 2 * SUBS, wide_cols - LANES
    row_start = lax.axis_index("gx") * block_rows
    col_start = lax.axis_index("gy") * block_cols
    rows_total = lax.axis_size("gx") * block_rows
    cols_total = lax.axis_size("gy") * block_cols
    wide = (wide_rows, wide_cols)
    row_ids = iota(wide, 0)
    row_ids = row_start + jnp.where(row_ids >= wide_rows - SUBS, row_ids - wide_rows, row_ids)
    row_ids = jnp.where(row_ids < 0, row_ids + rows_total, row_ids)
    row_ids = jnp.where(row_ids >= rows_total, row_ids - rows_total, row_ids)
    col_ids = iota(wide, 1)
    col_ids = col_start + jnp.where(col_ids >= wide_cols - LANES // 2, col_ids - wide_cols, col_ids)
    col_ids = jnp.where(col_ids < 0, col_ids + cols_total, col_ids)
    col_ids = jnp.where(col_ids >= cols_total, col_ids - cols_total, col_ids)
    for k in range(count):
        probes_ref[k] = sign_bits(seeds_ref[:, k : k + 1], row_ids, col_ids)


def stencil(v, coefs):
    centre, cx, cx_before, cy, cy_before = coefs
    return (
        centre[...] * v
        - cx[...] * roll(v, -1, 0)
        - cx_before[...] * roll(v, 1, 0)
        - cy[...] * roll(v, -1, 1)
        - cy_before[...] * roll(v, 1, 1)
    )


def image_kernel(
    live_ref, cells_ref, weight_ref, d_ref, cx_ref, cy_ref, obs_ref,
    above_ref, left_ref, corner_ref, below_ref, right_ref, probes_ref,
    image_ref, sums_ref, fix_ref,
    centre, cx_wide, cx_before, cy_wide, cy_before,
):
    count, block_rows, block_cols = obs_ref.shape
    wide_rows, wide_cols = centre.shape
    own = slice(0, block_rows), slice(0, block_cols)
    under, over = slice(block_rows, block_rows + SUBS), slice(block_rows + SUBS, wide_rows)
    main, side = slice(0, block_cols), slice(block_cols, wide_cols)
    left = expand(left_ref[...], block_rows, side_width(count))
    right = expand(right_ref[...], block_rows, BACK_WIDTH)
    corner = corner_ref[...]
    above = above_ref[SUBS : 2 * SUBS]
    below = below_ref[...]
    lane = iota((block_rows, LANES), 1)
    tile_lane = iota((SUBS, LANES), 1)
    nothing = jnp.zeros((SUBS, LANES), F32)
    for target, block, top, bottom, left_steps, right_steps, corner_steps in (
        (centre, d_ref, above, roll(below, -1, 0), 5, 2, 0),
        (cx_wide, cx_ref, above_ref[:SUBS], below, 9, 3, HALO),
        (cy_wide, cy_ref, roll(above, 4, 0), roll(below, -2, 0), 0, 1, 2 * HALO),
    ):
        target[own] = block[...]
        target[over, main] = top
        target[under, main] = bottom
        near = roll(left, left_steps, 1) if left_steps else left
        near = jnp.where(lane >= LANES - HALO, near, 0.0)
        target[own[0], side] = jnp.where(lane == 0, roll(right, right_steps, 1), near)
        tile = roll(corner, corner_steps, 1) if corner_steps else corner
        target[over, side] = jnp.where(tile_lane >= LANES - HALO, tile, 0.0)
        target[under, side] = nothing
    cx, cy = cx_wide[...], cy_wide[...]
    cx_up, cy_left = roll(cx, 1, 0), roll(cy, 1, 1)
    cx_before[...] = cx_up
    cy_before[...] = cy_left
    centre[...] = centre[...] + (cx + cx_up) + (cy + cy_left)
    coefs = (centre, cx_wide, cx_before, cy_wide, cy_before)

    slots = cells_ref.shape[1]
    cells = cells_ref[...]
    row_hot, col_hot = one_hots(cells, block_rows, block_cols)
    live = live_ref[...]
    sub = iota((SUBS, block_cols), 0)
    tile_sub = iota((SUBS, LANES), 0)
    wide_sub = iota((SUBS, wide_cols), 0)
    wide_lane = iota((1, wide_cols), 1)
    kept = jnp.where((wide_lane < block_cols - 2) | (wide_lane >= wide_cols - 2), 1.0, 0.0)

    def summed(value):
        line = jnp.sum(value[: block_rows - SUBS], 0, keepdims=True)
        edge = jnp.where(wide_sub < SUBS - 2, value[block_rows - SUBS : block_rows], value[over])
        return (line + jnp.sum(edge, 0, keepdims=True)) * kept

    stack, lines, first_miss, second_miss = [], [], [], []
    for k in range(count):
        probe = probes_ref[k]
        once = stencil(probe, coefs)
        near = jnp.where(lane >= LANES - 3, roll(left, 13 + 3 * k, 1), 0.0)
        tile = above_ref[(2 + k // 2) * SUBS : (3 + k // 2) * SUBS]
        tile = jnp.where(sub >= SUBS - 3, roll(tile, 3, 0) if k % 2 else tile, 0.0)
        seen_corner = roll(corner, HALO * (3 + k), 1)
        seen_corner = jnp.where((tile_lane >= LANES - 3) & (tile_sub >= SUBS - 3), seen_corner, 0.0)
        seen = jnp.concatenate(
            [
                jnp.concatenate([obs_ref[k], near], 1),
                jnp.zeros((SUBS, wide_cols), F32),
                jnp.concatenate([tile, seen_corner], 1),
            ],
            0,
        )
        image = stencil(once, coefs) + seen
        applied = stencil(image, coefs)
        lines.append([summed(probe * image), summed(image * image), summed(applied * applied)])
        image = image[own]
        image_ref[k] = image
        stack.extend(pieces(image))
        low = block_rows
        first_miss.append(
            cx_ref[low - 1 : low, 0:1]
            * (probe[low : low + 1, wide_cols - 1 : wide_cols] - probe[low : low + 1, 0:1])
        )
        far = slice(block_cols, block_cols + 1)
        second_miss.append(
            cy_ref[0:1, block_cols - 1 : block_cols]
            * (probe[wide_rows - 1 : wide_rows, far] - probe[0:1, far])
        )
    found = jnp.dot(jnp.concatenate(stack, 0), col_hot, preferred_element_type=F32)
    sampled = []
    for k in range(count):
        base = 3 * k * block_rows
        high, middle, low = (
            found[base + i * block_rows : base + (i + 1) * block_rows] for i in range(3)
        )
        sampled.append(jnp.sum(((low + middle) + high) * row_hot, 0, keepdims=True) * live)
    first_hot = jnp.where(cells == (block_rows - 1) * block_cols, live, 0.0)
    second_hot = jnp.where(cells == block_cols - 1, live, 0.0)
    spare = -(count + 2) % SUBS
    points = sampled + [first_hot, second_hot] + [jnp.zeros((spare, slots), F32)] * (spare > 0)
    points = jnp.concatenate(points, 0)
    weighted = jnp.dot(
        points, weight_ref[...], precision=lax.Precision.HIGHEST, preferred_element_type=F32
    )

    def total(value):
        return jnp.sum(value, 1, keepdims=True)

    with_points = total(points * weighted)
    with_first = total(points * weighted[count : count + 1] + weighted * first_hot)
    with_second = total(points * weighted[count + 1 : count + 2] + weighted * second_hot)
    out_lane = iota((1, LANES), 1)
    row = jnp.zeros((1, LANES), F32)
    fix = jnp.zeros((1, LANES), F32)
    for k in range(count):
        one, two = first_miss[k], second_miss[k]
        values = [total(line) for line in lines[k]]
        values[2] = values[2] + with_points[k : k + 1]
        values.append(one * with_first[k : k + 1])
        values.append(two * with_second[k : k + 1])
        values.append(one * one * with_points[count : count + 1])
        values.append(two * two * with_points[count + 1 : count + 2])
        values.append(one * two * with_first[count + 1 : count + 2])
        for i, value in enumerate(values):
            row = jnp.where(out_lane == i * count + k, value, row)
        fix = jnp.where(out_lane == k, one, jnp.where(out_lane == count + k, two, fix))
    row = jnp.where(out_lane == 8 * count, cy_ref[0:1, block_cols - 1 : block_cols], row)
    row = jnp.where(out_lane == 8 * count + 1, cx_ref[block_rows - 1 : block_rows, 0:1], row)
    sums_ref[...] = jnp.broadcast_to(row[None], sums_ref.shape)
    fix_ref[...] = fix


def finish_kernel(sums_ref, probes_ref, image_ref, fix_ref, solution_ref, trace_ref):
    count, block_rows, block_cols = image_ref.shape
    across = lax.axis_size("gy")
    devices = sums_ref.shape[0]
    rows = jnp.sum(sums_ref[...], 1)
    member = iota((devices, 1), 0)
    place = lax.rem(member, across)
    lower = roll(rows, -across, 0)
    lower = jnp.where(place == 0, roll(lower, 1 - across, 0), roll(lower, 1, 0))
    upper = roll(rows, across, 0)
    upper = jnp.where(place == across - 1, roll(upper, across - 1, 0), roll(upper, -1, 0))
    one = lower[:, 8 * count : 8 * count + 1]
    two = upper[:, 8 * count + 1 : 8 * count + 2]
    part = [roll(rows, -i * count, 1) if i else rows for i in range(8)]
    third = part[2] + one * (part[3] + one * part[5] + two * part[7]) + two * (part[4] + two * part[6])

    cells_total = float(block_rows * block_cols * devices)
    first = jnp.sum(part[0], 0, keepdims=True)
    second = jnp.sum(part[1], 0, keepdims=True)
    third = jnp.sum(third, 0, keepdims=True)
    step = cells_total / first
    growth = step * step * second * (1.0 / cells_total)
    ratio = growth - 1.0
    bend = step * step * step * third * (1.0 / cells_total) - growth * growth
    next_step = step * ratio / bend
    on_probe = step + next_step * growth
    on_image = step * next_step
    used = iota(first.shape, 1) < count
    trace = jnp.where(used, step + next_step * ratio, 0.0)
    trace_ref[...] = jnp.sum(trace, 1, keepdims=True) * (cells_total / count)

    mine = member == lax.axis_index("gx") * across + lax.axis_index("gy")
    fix = fix_ref[...]
    change = on_image * fix * jnp.sum(jnp.where(mine, one, 0.0), 0, keepdims=True)
    other = on_image * roll(fix, -count, 1) * jnp.sum(jnp.where(mine, two, 0.0), 0, keepdims=True)
    tile_sub, tile_lane = iota((SUBS, LANES), 0), iota((SUBS, LANES), 1)
    low_left = (tile_sub == SUBS - 1) & (tile_lane == 0)
    high_right = (tile_sub == 0) & (tile_lane == LANES - 1)
    tail = slice(block_rows - SUBS, block_rows)
    last = slice(block_cols - LANES, block_cols)
    for k in range(count):
        here = slice(k, k + 1)
        value = (
            on_probe[:, here] * probes_ref[k, :block_rows, :block_cols]
            - on_image[:, here] * image_ref[k]
        )
        solution_ref[k] = value
        solution_ref[k, tail, :LANES] = solution_ref[k, tail, :LANES] - jnp.where(
            low_left, change[:, here], 0.0
        )
        solution_ref[k, :SUBS, last] = solution_ref[k, :SUBS, last] - jnp.where(
            high_right, other[:, here], 0.0
        )


def per_device(
    probe_seeds, damping, coupling_x, coupling_y, sensor_count, sensor_cells, obs_weight
):
    block_rows, block_cols = damping.shape
    count = probe_seeds.shape[0]
    slots = obs_weight.shape[-1]
    wide_rows, wide_cols = block_rows + 2 * SUBS, block_cols + LANES
    devices = lax.axis_size("gx") * lax.axis_size("gy")
    full = jax.ShapeDtypeStruct

    def call(kernel, args, outs, scratch=(), scalars=0):
        return pl.pallas_call(
            kernel,
            out_shape=outs,
            in_specs=[SMEM] * scalars + [VMEM] * (len(args) - scalars),
            out_specs=[VMEM] * len(outs),
            scratch_shapes=scratch,
        )(*args)

    def space(*shape):
        return pltpu.VMEM(shape, F32)

    block = space(block_rows, block_cols)
    blocks = space(count, block_rows, block_cols)
    seeds = probe_seeds.reshape(1, count)
    outs = call(
        start_kernel,
        (
            sensor_count,
            seeds,
            sensor_cells.reshape(1, slots),
            obs_weight.reshape(slots, slots),
            damping,
            coupling_x,
            coupling_y,
        ),
        [
            pltpu.VMEM((1, slots), jnp.int32),
            space(slots, slots),
            block,
            block,
            block,
            blocks,
            space(1, slots),
            space(SUBS * (2 + (count + 1) // 2), block_cols),
            space(compact_rows(block_rows, side_width(count)), LANES),
            space(SUBS, LANES),
            space(SUBS, block_cols),
            space(compact_rows(block_rows, BACK_WIDTH), LANES),
        ],
        scalars=1,
    )
    cells, weight, *coefs, observed, live = on_chip(*outs[:7])
    rows_next, cols_next, diag_next, rows_back, cols_back = outs[7:]
    above = shifted(rows_next, "gx", 1)
    corner = shifted_both(diag_next)
    left = shifted(cols_next, "gy", 1)
    below = shifted(rows_back, "gx", -1)
    right = shifted(cols_back, "gy", -1)

    probes, = on_chip(
        *call(probes_kernel, (seeds,), [space(count, wide_rows, wide_cols)])
    )
    image, sums, fix = call(
        image_kernel,
        (
            live,
            cells,
            weight,
            *coefs,
            observed,
            *on_chip(above, left, corner, below, right),
            probes,
        ),
        [blocks, space(devices, 1, LANES), space(1, LANES)],
        [space(wide_rows, wide_cols)] * 5,
    )
    sums = lax.all_to_all(sums, ("gx", "gy"), 0, 0, tiled=True)
    solved, trace = call(
        finish_kernel,
        (*on_chip(sums), probes, *on_chip(image, fix)),
        [full((count, block_rows, block_cols), F32), full((1, 1), F32)],
    )
    return solved, trace[0, 0]


def solution(mesh):
    placed = (
        P(),
        P("gx", "gy"),
        P("gx", "gy"),
        P("gx", "gy"),
        P("gx", "gy"),
        P("gx", "gy", None),
        P("gx", "gy", None, None),
    )

    return jax.shard_map(
        per_device,
        mesh=mesh,
        in_specs=placed,
        out_specs=(P(None, "gx", "gy"), P()),
        check_vma=False,
    )
```

time: 30.9 us -> 28.2 us (0.913)
  waiting for transfers between devices: 8.4 us -> 4.24 us
  Pallas kernels: 4.5 us -> 5.64 us
  blocking collectives: 8.87 us -> 9.21 us
    ppermute x6 -> x4, waiting for transfers between devices: 8.4 us -> 0.01 us  [shifted(): return lax.ppermute(value, axis, pairs)]
    ppermute x0 -> x1, waiting for transfers between devices: none -> 4.23 us  [shifted_both(): return lax.ppermute(value, ('gx', 'gy'), pairs)]
    pallas_call x5 -> x4, Pallas kernels: 4.5 us -> 5.64 us  [call(): pl.pallas_call(kernel, out_shape=outs, in_specs=[SMEM] * scalars + [VMEM]...]
    all_to_all x1, blocking collectives: 8.87 us -> 9.21 us  [per_device(): sums = lax.all_to_all(sums, ('gx', 'gy'), 0, 0, tiled=True)]
    ppermute x6 -> x4, starting transfers between devices: 7.67 us -> 7.59 us  [shifted(): return lax.ppermute(value, axis, pairs)]
  transfers between devices with their start and end apart: 6 -> 5, of which waited for: 4 -> 1; matrix products, arithmetic and copies ran while one was open for 0% -> 0% of each run, Pallas kernels for 3% -> 4%
where the time goes in v3:
time: 28.2 us; the launch traced here: 28 us
  blocking collectives  9.21 us (33%)
  starting transfers between devices  7.59 us (27%)
  Pallas kernels  5.64 us (20%)
  waiting for transfers between devices  4.24 us (15%)
  between operations  1.31 us (5%)
    all_to_all x1, blocking collectives, per_device(): sums = lax.all_to_all(sums, ('gx', 'gy'), 0, 0, tiled=True)  9.21 us
    ppermute x4, starting transfers between devices, shifted(): return lax.ppermute(value, axis, pairs)  7.59 us
    pallas_call x4, Pallas kernels, call(): pl.pallas_call(kernel, out_shape=outs, in_specs=[SMEM] * scalars + [VMEM]...  5.64 us
    ppermute x1, waiting for transfers between devices, shifted_both(): return lax.ppermute(value, ('gx', 'gy'), pairs)  4.23 us
  transfers between devices with their start and end apart: 5, of which 1 were waited for; matrix products, arithmetic and copies ran while one was open for 0% of the time, Pallas kernels for 4%

profile of v3, /device:TPU:0, one launch (start us, length us, event | category | flops | bytes accessed | tf_op | source)
XLA Modules:
  0.0 28.0 jit_solution(3228313800428201620)
XLA Ops:
  1.3 1.9 %shard_map.86 = (s32[1,256]{1,0:T(1,128)S(1)}, f32[256,256]{1,0:T(8,128)S(1)}, f32[64,256]{1,0:T(8,128)S(1)}, f32[64,256]{1,0:T(8,128)S(1)}, f32[64,256]{1,0:T(8...) custom-call(s32[1,1]{1,0:T(1,128)S(6)} %copy.9.number_ref, ...), custom_call_target="tpu_custom_call" | custom-call | tf_op jit(solution)/shard_map/pallas_call | solution.py:423
  3.1 3.0 %collective-permute-start = (f32[32,256]{1,0:T(8,128)S(1)}, f32[32,256]{1,0:T(8,128)S(1)}, u32[]{:S(2)}, u32[]{:S(2)}) collective-permute-start(f32[32,256]{1,0:T(8,128)S(1)} %get-tuple-element.26), channel_id=1, source_target_pairs={{0,4},{4,8},{8,12},{12,16},{16,20},{20,24},{24,28},{28,0},{1,5},{5... | collective-permute-start | bytes 98312 | tf_op jit(solution)/shard_map/ppermute | solution.py:20
  6.2 0.0 collective-permute-start.1
  6.2 3.2 %collective-permute-start.3 = (f32[8,256]{1,0:T(8,128)S(1)}, f32[8,256]{1,0:T(8,128)S(1)}, u32[]{:S(2)}, u32[]{:S(2)}) collective-permute-start(f32[8,256]{1,0:T(8,128)S(1)} %get-tuple-element.29), channel_id=1, source_target_pairs={{0,28},{4,0},{8,4},{12,8},{16,12},{20,16},{24,20},{28,24},{1,29},{... | collective-permute-start | bytes 24584 | tf_op jit(solution)/shard_map/ppermute | solution.py:20
  9.3 0.0 collective-permute-start.2
  9.3 1.4 %collective-permute-start.4 = (f32[8,128]{1,0:T(8,128)S(1)}, f32[8,128]{1,0:T(8,128)S(1)}, u32[]{:S(2)}, u32[]{:S(2)}) collective-permute-start(f32[8,128]{1,0:T(8,128)S(1)} %get-tuple-element.30), channel_id=1, source_target_pairs={{0,3},{1,0},{2,1},{3,2},{4,7},{5,4},{6,5},{7,6},{8,11},{9,8},{10,9... | collective-permute-start | bytes 12296 | tf_op jit(solution)/shard_map/ppermute | solution.py:20
  10.7 1.0 %shard_map.87.probes_ref = f32[4,80,384]{2,1,0:T(8,128)S(1)} custom-call(s32[1,4]{1,0:T(1,128)} %bitcast.6), custom_call_target="tpu_custom_call" | custom-call | tf_op jit(solution)/shard_map/pallas_call | solution.py:423
  11.7 4.2 %collective-permute-done.2.corner_ref = f32[8,128]{1,0:T(8,128)S(1)} collective-permute-done((f32[8,128]{1,0:T(8,128)S(1)}, f32[8,128]{1,0:T(8,128)S(1)}, u32[]{:S(2)}, u32[]{:S(2)}) %collective-permute-start.2) | collective-permute-done | bytes 4128 | tf_op jit(solution)/shard_map/ppermute | solution.py:30
  16.0 0.0 collective-permute-done.4.right_ref
  16.0 0.0 collective-permute-done.1.left_ref
  16.0 0.0 collective-permute-done.3.below_ref
  16.0 0.0 collective-permute-done.above_ref
  16.0 1.8 %shard_map.88 = (f32[4,64,256]{2,1,0:T(8,128)S(1)}, f32[32,1,128]{2,1,0:T(1,128)S(1)}, f32[1,128]{1,0:T(1,128)S(1)}) custom-call(f32[1,256]{1,0:T(1,128)S(1)} %get-tuple-element.19.live_ref, s32[1,256]{1,0:T(1,128)S(1)} %get-tuple-element.20.cells_ref, f32[256,256]{1,0:T(8,128)S(1)} %get-tuple-element.21.weight_ref, f32[64,256]{1,0:T(8,128)S(1)} %get-tuple-element.22.d_ref, ...), custom_call_target="tpu_custom_call" | custom-call | tf_op jit(solution)/shard_map/pallas_call | solution.py:423
  17.8 9.2 %all_to_all.5.sums_ref = f32[32,1,128]{2,1,0:T(1,128)S(1)} all-to-all(f32[32,1,128]{2,1,0:T(1,128)S(1)} %get-tuple-element.31), channel_id=1, replica_groups=mesh['gx'=8,'gy'=4] {'gx','gy'}, dimensions={0} | all-to-all | bytes 32768 | tf_op jit(solution)/shard_map/all_to_all | solution.py:489
  27.0 1.0 %shard_map.89 = (f32[4,64,256]{2,1,0:T(8,128)}, f32[1,1]{1,0:T(1,128)}) custom-call(f32[32,1,128]{2,1,0:T(1,128)S(1)} %all_to_all.5.sums_ref, f32[4,80,384]{2,1,0:T(8,128)S(1)} %shard_map.87.probes_ref, f32[4,64,256]{2,1,0:T(8,128)S(1)} %get-tuple-element.32.image_ref, f32[1,128]{1,0:T(1,128)S(1)} %get-tuple-element.33.fix_ref), custom_call_target="tpu_custom_call" | custom-call | tf_op jit(solution)/shard_map/pallas_call | solution.py:423
Async XLA Ops:
  3.1 12.8 %collective-permute-start = (f32[32,256]{1,0:T(8,128)S(1)}, f32[32,256]{1,0:T(8,128)S(1)}, u32[]{:S(2)}, u32[]{:S(2)}) collective-permute-start(f32[32,256]{1,0:T(8,128)S(1)} %get-tuple-element.26), channel_id=1, source_target_pairs={{0,4},{4,8},{8,12},{12,16},{16,20},{20,24},{24,28},{28,0},{1,5},{5... | collective-permute-start | bytes 98312 | tf_op jit(solution)/shard_map/ppermute | solution.py:20
  6.2 9.8 %collective-permute-start.1 = (f32[16,128]{1,0:T(8,128)S(1)}, f32[16,128]{1,0:T(8,128)S(1)}, u32[]{:S(2)}, u32[]{:S(2)}) collective-permute-start(f32[16,128]{1,0:T(8,128)S(1)} %get-tuple-element.27), channel_id=1, source_target_pairs={{0,1},{1,2},{2,3},{3,0},{4,5},{5,6},{6,7},{7,4},{8,9},{9,10},{10,1... | collective-permute-start | bytes 24584 | tf_op jit(solution)/shard_map/ppermute | solution.py:20
  6.2 9.8 %collective-permute-start.3 = (f32[8,256]{1,0:T(8,128)S(1)}, f32[8,256]{1,0:T(8,128)S(1)}, u32[]{:S(2)}, u32[]{:S(2)}) collective-permute-start(f32[8,256]{1,0:T(8,128)S(1)} %get-tuple-element.29), channel_id=1, source_target_pairs={{0,28},{4,0},{8,4},{12,8},{16,12},{20,16},{24,20},{28,24},{1,29},{... | collective-permute-start | bytes 24584 | tf_op jit(solution)/shard_map/ppermute | solution.py:20
  9.3 6.6 %collective-permute-start.2 = (f32[8,128]{1,0:T(8,128)S(1)}, f32[8,128]{1,0:T(8,128)S(1)}, u32[]{:S(2)}, u32[]{:S(2)}) collective-permute-start(f32[8,128]{1,0:T(8,128)S(1)} %get-tuple-element.28), channel_id=1, source_target_pairs={{0,5},{1,6},{2,7},{3,4},{4,9},{5,10},{6,11},{7,8},{8,13},{9,14},{1... | collective-permute-start | bytes 12296 | tf_op jit(solution)/shard_map/ppermute | solution.py:30
  9.3 6.6 %collective-permute-start.4 = (f32[8,128]{1,0:T(8,128)S(1)}, f32[8,128]{1,0:T(8,128)S(1)}, u32[]{:S(2)}, u32[]{:S(2)}) collective-permute-start(f32[8,128]{1,0:T(8,128)S(1)} %get-tuple-element.30), channel_id=1, source_target_pairs={{0,3},{1,0},{2,1},{3,2},{4,7},{5,4},{6,5},{7,6},{8,11},{9,8},{10,9... | collective-permute-start | bytes 12296 | tf_op jit(solution)/shard_map/ppermute | solution.py:20

commit v4 on v3

--- a/solution.py
+++ b/solution.py
@@ -52,10 +52,11 @@
 
 def pieces(value):
     high = value.astype(BF16)
-    rest = value - high.astype(F32)
-    middle = rest.astype(BF16)
-    low = (rest - middle.astype(F32)).astype(BF16)
-    return high, middle, low
+    return high, (value - high.astype(F32)).astype(BF16)
+
+
+def dot(left, right):
+    return jnp.dot(left, right, preferred_element_type=F32)
 
 
 def split_cells(cells, block_cols):
@@ -113,7 +114,7 @@
 
 def start_kernel(
     number_ref, seeds_ref, cells_in, weight_in, d_in, cx_in, cy_in,
-    cells_ref, weight_ref, d_ref, cx_ref, cy_ref, obs_ref, live_ref,
+    seeds_out, cells_ref, high_ref, low_ref, d_ref, cx_ref, cy_ref, obs_ref, live_ref,
     rows_next_ref, cols_next_ref, diag_next_ref, rows_back_ref, cols_back_ref,
 ):
     count, block_rows, block_cols = obs_ref.shape
@@ -121,9 +122,10 @@
     col_start = lax.axis_index("gy") * block_cols
     slots = cells_in.shape[1]
     cells = cells_in[...]
-    weight = weight_in[...]
+    seeds_out[...] = seeds_ref[...]
     cells_ref[...] = cells
-    weight_ref[...] = weight
+    weight_high, weight_low = pieces(weight_in[...])
+    high_ref[...], low_ref[...] = weight_high, weight_low
     rows, cols = split_cells(cells, block_cols)
     padded = count + -count % SUBS
     which = iota((padded, slots), 0)
@@ -132,10 +134,8 @@
         seeds = jnp.where(which == k, seeds_ref[:, k : k + 1], seeds)
     live = jnp.where(iota((1, slots), 1) < number_ref[0, 0], 1.0, 0.0)
     live_ref[...] = live
-    sampled = sign_bits(seeds, rows + row_start, cols + col_start) * live
-    weighted = (
-        jnp.dot(sampled, weight, precision=lax.Precision.HIGHEST, preferred_element_type=F32) * live
-    )
+    sampled = (sign_bits(seeds, rows + row_start, cols + col_start) * live).astype(BF16)
+    weighted = (dot(sampled, weight_high) + dot(sampled, weight_low)) * live
     row_hot, col_hot = one_hots(cells, block_rows, block_cols)
     parts = pieces(weighted)
     stack = [
@@ -146,11 +146,9 @@
     )
     observed = []
     for k in range(count):
-        base = 3 * k * block_rows
-        high, middle, low = (
-            spread[base + i * block_rows : base + (i + 1) * block_rows] for i in range(3)
-        )
-        observed.append((low + middle) + high)
+        base = 2 * k * block_rows
+        high, low = (spread[base + i * block_rows : base + (i + 1) * block_rows] for i in range(2))
+        observed.append(low + high)
         obs_ref[k] = observed[k]
 
     d, cx, cy = d_in[...], cx_in[...], cy_in[...]
@@ -191,141 +189,213 @@
     cols_back_ref[...] = compact(back, BACK_WIDTH)
 
 
+TOP = 2 * SUBS
+
+
 def probes_kernel(seeds_ref, probes_ref):
-    count, wide_rows, wide_cols = probes_ref.shape
-    block_rows, block_cols = wide_rows - 2 * SUBS, wide_cols - LANES
+    count, tiles, wide_rows, _ = probes_ref.shape
+    block_rows, block_cols = wide_rows - 2 * TOP, (tiles - 1) * LANES
     row_start = lax.axis_index("gx") * block_rows
     col_start = lax.axis_index("gy") * block_cols
     rows_total = lax.axis_size("gx") * block_rows
     cols_total = lax.axis_size("gy") * block_cols
-    wide = (wide_rows, wide_cols)
-    row_ids = iota(wide, 0)
-    row_ids = row_start + jnp.where(row_ids >= wide_rows - SUBS, row_ids - wide_rows, row_ids)
+    row_ids = row_start - TOP + iota((wide_rows, LANES), 0)
     row_ids = jnp.where(row_ids < 0, row_ids + rows_total, row_ids)
     row_ids = jnp.where(row_ids >= rows_total, row_ids - rows_total, row_ids)
-    col_ids = iota(wide, 1)
-    col_ids = col_start + jnp.where(col_ids >= wide_cols - LANES // 2, col_ids - wide_cols, col_ids)
-    col_ids = jnp.where(col_ids < 0, col_ids + cols_total, col_ids)
-    col_ids = jnp.where(col_ids >= cols_total, col_ids - cols_total, col_ids)
-    for k in range(count):
-        probes_ref[k] = sign_bits(seeds_ref[:, k : k + 1], row_ids, col_ids)
-
-
-def stencil(v, coefs):
-    centre, cx, cx_before, cy, cy_before = coefs
-    return (
-        centre[...] * v
-        - cx[...] * roll(v, -1, 0)
-        - cx_before[...] * roll(v, 1, 0)
-        - cy[...] * roll(v, -1, 1)
-        - cy_before[...] * roll(v, 1, 1)
-    )
+    for j in range(tiles):
+        col_ids = iota((1, LANES), 1)
+        if j == tiles - 1:
+            col_ids = jnp.where(col_ids < LANES // 2, col_ids + block_cols, col_ids - LANES)
+        else:
+            col_ids = col_ids + j * LANES
+        col_ids = col_start + col_ids
+        col_ids = jnp.where(col_ids < 0, col_ids + cols_total, col_ids)
+        col_ids = jnp.where(col_ids >= cols_total, col_ids - cols_total, col_ids)
+        for k in range(count):
+            probes_ref[k, j] = sign_bits(seeds_ref[:, k : k + 1], row_ids, col_ids)
+
+
+def side_step(tiles, steps):
+    lane = iota(tiles[0].shape, 1)
+    turned = [roll(tile, -steps, 1) for tile in tiles]
+    if steps > 0:
+        return [
+            jnp.where(lane == LANES - 1, turned[(j + 1) % len(tiles)], turned[j])
+            for j in range(len(tiles))
+        ]
+    return [jnp.where(lane == 0, turned[j - 1], turned[j]) for j in range(len(tiles))]
 
 
 def image_kernel(
-    live_ref, cells_ref, weight_ref, d_ref, cx_ref, cy_ref, obs_ref,
+    live_ref, cells_ref, high_ref, low_ref, d_ref, cx_ref, cy_ref, obs_ref,
     above_ref, left_ref, corner_ref, below_ref, right_ref, probes_ref,
     image_ref, sums_ref, fix_ref,
-    centre, cx_wide, cx_before, cy_wide, cy_before,
+    centre, cx_wide, cy_wide, cy_before, seen, once, image,
 ):
     count, block_rows, block_cols = obs_ref.shape
-    wide_rows, wide_cols = centre.shape
-    own = slice(0, block_rows), slice(0, block_cols)
-    under, over = slice(block_rows, block_rows + SUBS), slice(block_rows + SUBS, wide_rows)
-    main, side = slice(0, block_cols), slice(block_cols, wide_cols)
+    tiles, _, _ = centre.shape
+    side = tiles - 1
+    own = slice(TOP, TOP + block_rows)
+    over, under = slice(TOP - SUBS, TOP), slice(TOP + block_rows, TOP + block_rows + SUBS)
     left = expand(left_ref[...], block_rows, side_width(count))
     right = expand(right_ref[...], block_rows, BACK_WIDTH)
     corner = corner_ref[...]
     above = above_ref[SUBS : 2 * SUBS]
     below = below_ref[...]
     lane = iota((block_rows, LANES), 1)
-    tile_lane = iota((SUBS, LANES), 1)
+    sub, tile_lane = iota((SUBS, LANES), 0), iota((SUBS, LANES), 1)
     nothing = jnp.zeros((SUBS, LANES), F32)
+
+    def lanes_of(j):
+        return slice(j * LANES, (j + 1) * LANES)
+
     for target, block, top, bottom, left_steps, right_steps, corner_steps in (
         (centre, d_ref, above, roll(below, -1, 0), 5, 2, 0),
         (cx_wide, cx_ref, above_ref[:SUBS], below, 9, 3, HALO),
         (cy_wide, cy_ref, roll(above, 4, 0), roll(below, -2, 0), 0, 1, 2 * HALO),
     ):
-        target[own] = block[...]
-        target[over, main] = top
-        target[under, main] = bottom
+        for j in range(side):
+            target[j, own] = block[:, lanes_of(j)]
+            target[j, over] = top[:, lanes_of(j)]
+            target[j, under] = bottom[:, lanes_of(j)]
         near = roll(left, left_steps, 1) if left_steps else left
         near = jnp.where(lane >= LANES - HALO, near, 0.0)
-        target[own[0], side] = jnp.where(lane == 0, roll(right, right_steps, 1), near)
+        target[side, own] = jnp.where(lane == 0, roll(right, right_steps, 1), near)
         tile = roll(corner, corner_steps, 1) if corner_steps else corner
-        target[over, side] = jnp.where(tile_lane >= LANES - HALO, tile, 0.0)
-        target[under, side] = nothing
-    cx, cy = cx_wide[...], cy_wide[...]
-    cx_up, cy_left = roll(cx, 1, 0), roll(cy, 1, 1)
-    cx_before[...] = cx_up
-    cy_before[...] = cy_left
-    centre[...] = centre[...] + (cx + cx_up) + (cy + cy_left)
-    coefs = (centre, cx_wide, cx_before, cy_wide, cy_before)
+        target[side, over] = jnp.where(tile_lane >= LANES - HALO, tile, 0.0)
+        target[side, under] = nothing
+    for k in range(count):
+        tile = above_ref[(2 + k // 2) * SUBS : (3 + k // 2) * SUBS]
+        tile = roll(tile, 3, 0) if k % 2 else tile
+        for j in range(side):
+            seen[k, j, own] = obs_ref[k, :, lanes_of(j)]
+            seen[k, j, over] = jnp.where(sub >= SUBS - 3, tile[:, lanes_of(j)], 0.0)
+        seen[k, side, own] = jnp.where(lane >= LANES - 3, roll(left, 13 + 3 * k, 1), 0.0)
+        tile = roll(corner, HALO * (3 + k), 1)
+        seen[k, side, over] = jnp.where((tile_lane >= LANES - 3) & (sub >= SUBS - 3), tile, 0.0)
+
+    def rows_at(start, steps=0):
+        return pl.ds(start + steps, SUBS)
+
+    def prepare(i, carry):
+        start = i * SUBS
+        here = rows_at(start)
+        cy = [cy_wide[j, here] for j in range(tiles)]
+        cy_left = side_step(cy, -1)
+        for j in range(tiles):
+            cy_before[j, here] = cy_left[j]
+            cx_pair = cx_wide[j, here] + cx_wide[j, rows_at(start, -1)]
+            centre[j, here] = centre[j, here] + cx_pair + (cy[j] + cy_left[j])
+        return carry
+
+    def stencil(field, k, start, coefs):
+        here = rows_at(start)
+        v = [field[k, j, here] for j in range(tiles)]
+        ahead, behind = side_step(v, 1), side_step(v, -1)
+        result = []
+        for j in range(tiles):
+            middle, cx, cx_up, cy, cy_left = coefs[j]
+            result.append(
+                middle * v[j]
+                - cx * field[k, j, rows_at(start, 1)]
+                - cx_up * field[k, j, rows_at(start, -1)]
+                - cy * ahead[j]
+                - cy_left * behind[j]
+            )
+        return result, v
+
+    def coefs_at(start):
+        here = rows_at(start)
+        return [
+            (
+                centre[j, here],
+                cx_wide[j, here],
+                cx_wide[j, rows_at(start, -1)],
+                cy_wide[j, here],
+                cy_before[j, here],
+            )
+            for j in range(tiles)
+        ]
+
+    def first(i, carry):
+        start = i * SUBS
+        coefs = coefs_at(start)
+        for k in range(count):
+            result, _ = stencil(probes_ref, k, start, coefs)
+            for j in range(tiles):
+                once[k, j, rows_at(start)] = result[j]
+        return carry
+
+    def second(i, carry):
+        start = i * SUBS
+        coefs = coefs_at(start)
+        for k in range(count):
+            result, _ = stencil(once, k, start, coefs)
+            for j in range(tiles):
+                image[k, j, rows_at(start)] = result[j] + seen[k, j, rows_at(start)]
+        return carry
+
+    def products(start):
+        coefs = coefs_at(start)
+        terms = []
+        for k in range(count):
+            applied, q = stencil(image, k, start, coefs)
+            for j in range(tiles):
+                terms.append(probes_ref[k, j, rows_at(start)] * q[j])
+                terms.append(q[j] * q[j])
+                terms.append(applied[j] * applied[j])
+        return terms
+
+    def third(i, carry):
+        start = i * SUBS
+        return tuple(a + b for a, b in zip(carry, products(start)))
+
+    def loop(low, high, step, carry):
+        for i in range(low, high):
+            carry = step(i, carry)
+        return carry
+
+    lead, steps = TOP // SUBS, block_rows // SUBS
+    loop(lead - 1, lead + steps + 1, prepare, 0)
+    loop(lead - 1, lead + steps + 1, first, 0)
+    loop(lead - 1, lead + steps, second, 0)
+    edge = [
+        jnp.where(sub < SUBS - 2, a, b)
+        for a, b in zip(products(TOP + block_rows - SUBS), products(TOP - SUBS))
+    ]
+    lines = loop(lead, lead + steps - 1, third, tuple(edge))
 
     slots = cells_ref.shape[1]
     cells = cells_ref[...]
     row_hot, col_hot = one_hots(cells, block_rows, block_cols)
     live = live_ref[...]
-    sub = iota((SUBS, block_cols), 0)
-    tile_sub = iota((SUBS, LANES), 0)
-    wide_sub = iota((SUBS, wide_cols), 0)
-    wide_lane = iota((1, wide_cols), 1)
-    kept = jnp.where((wide_lane < block_cols - 2) | (wide_lane >= wide_cols - 2), 1.0, 0.0)
-
-    def summed(value):
-        line = jnp.sum(value[: block_rows - SUBS], 0, keepdims=True)
-        edge = jnp.where(wide_sub < SUBS - 2, value[block_rows - SUBS : block_rows], value[over])
-        return (line + jnp.sum(edge, 0, keepdims=True)) * kept
-
-    stack, lines, first_miss, second_miss = [], [], [], []
-    for k in range(count):
-        probe = probes_ref[k]
-        once = stencil(probe, coefs)
-        near = jnp.where(lane >= LANES - 3, roll(left, 13 + 3 * k, 1), 0.0)
-        tile = above_ref[(2 + k // 2) * SUBS : (3 + k // 2) * SUBS]
-        tile = jnp.where(sub >= SUBS - 3, roll(tile, 3, 0) if k % 2 else tile, 0.0)
-        seen_corner = roll(corner, HALO * (3 + k), 1)
-        seen_corner = jnp.where((tile_lane >= LANES - 3) & (tile_sub >= SUBS - 3), seen_corner, 0.0)
-        seen = jnp.concatenate(
-            [
-                jnp.concatenate([obs_ref[k], near], 1),
-                jnp.zeros((SUBS, wide_cols), F32),
-                jnp.concatenate([tile, seen_corner], 1),
-            ],
-            0,
+    stack, first_miss, second_miss = [], [], []
+    for k in range(count):
+        whole = jnp.concatenate([image[k, j, own] for j in range(side)], 1)
+        image_ref[k] = whole
+        stack.extend(pieces(whole))
+        low = TOP + block_rows
+        first_miss.append(
+            cx_ref[block_rows - 1 : block_rows, 0:1]
+            * (probes_ref[k, side, low : low + 1, LANES - 1 :] - probes_ref[k, 0, low : low + 1, 0:1])
         )
-        image = stencil(once, coefs) + seen
-        applied = stencil(image, coefs)
-        lines.append([summed(probe * image), summed(image * image), summed(applied * applied)])
-        image = image[own]
-        image_ref[k] = image
-        stack.extend(pieces(image))
-        low = block_rows
-        first_miss.append(
-            cx_ref[low - 1 : low, 0:1]
-            * (probe[low : low + 1, wide_cols - 1 : wide_cols] - probe[low : low + 1, 0:1])
-        )
-        far = slice(block_cols, block_cols + 1)
         second_miss.append(
             cy_ref[0:1, block_cols - 1 : block_cols]
-            * (probe[wide_rows - 1 : wide_rows, far] - probe[0:1, far])
+            * (probes_ref[k, side, TOP - 1 : TOP, 0:1] - probes_ref[k, side, TOP : TOP + 1, 0:1])
         )
-    found = jnp.dot(jnp.concatenate(stack, 0), col_hot, preferred_element_type=F32)
+    found = dot(jnp.concatenate(stack, 0), col_hot)
     sampled = []
     for k in range(count):
-        base = 3 * k * block_rows
-        high, middle, low = (
-            found[base + i * block_rows : base + (i + 1) * block_rows] for i in range(3)
-        )
-        sampled.append(jnp.sum(((low + middle) + high) * row_hot, 0, keepdims=True) * live)
+        base = 2 * k * block_rows
+        high, low = (found[base + i * block_rows : base + (i + 1) * block_rows] for i in range(2))
+        sampled.append(jnp.sum((low + high) * row_hot, 0, keepdims=True) * live)
     first_hot = jnp.where(cells == (block_rows - 1) * block_cols, live, 0.0)
     second_hot = jnp.where(cells == block_cols - 1, live, 0.0)
     spare = -(count + 2) % SUBS
     points = sampled + [first_hot, second_hot] + [jnp.zeros((spare, slots), F32)] * (spare > 0)
     points = jnp.concatenate(points, 0)
-    weighted = jnp.dot(
-        points, weight_ref[...], precision=lax.Precision.HIGHEST, preferred_element_type=F32
-    )
+    high, low = pieces(points)
+    weighted = dot(high, high_ref[...]) + (dot(low, high_ref[...]) + dot(high, low_ref[...]))
 
     def total(value):
         return jnp.sum(value, 1, keepdims=True)
@@ -338,7 +408,11 @@
     fix = jnp.zeros((1, LANES), F32)
     for k in range(count):
         one, two = first_miss[k], second_miss[k]
-        values = [total(line) for line in lines[k]]
+        values = []
+        for i in range(3):
+            line = [jnp.sum(lines[3 * (k * tiles + j) + i], 0, keepdims=True) for j in range(tiles)]
+            line[side - 1] = jnp.where(out_lane < LANES - 2, line[side - 1], line[side])
+            values.append(total(sum(line[:side])))
         values[2] = values[2] + with_points[k : k + 1]
         values.append(one * with_first[k : k + 1])
         values.append(two * with_second[k : k + 1])
@@ -396,10 +470,10 @@
     last = slice(block_cols - LANES, block_cols)
     for k in range(count):
         here = slice(k, k + 1)
-        value = (
-            on_probe[:, here] * probes_ref[k, :block_rows, :block_cols]
-            - on_image[:, here] * image_ref[k]
-        )
+        probe = [
+            probes_ref[k, j, TOP : TOP + block_rows] for j in range(block_cols // LANES)
+        ]
+        value = on_probe[:, here] * jnp.concatenate(probe, 1) - on_image[:, here] * image_ref[k]
         solution_ref[k] = value
         solution_ref[k, tail, :LANES] = solution_ref[k, tail, :LANES] - jnp.where(
             low_left, change[:, here], 0.0
@@ -415,7 +489,7 @@
     block_rows, block_cols = damping.shape
     count = probe_seeds.shape[0]
     slots = obs_weight.shape[-1]
-    wide_rows, wide_cols = block_rows + 2 * SUBS, block_cols + LANES
+    wide = (block_cols // LANES + 1, block_rows + 2 * TOP, LANES)
     devices = lax.axis_size("gx") * lax.axis_size("gy")
     full = jax.ShapeDtypeStruct
 
@@ -446,8 +520,10 @@
             coupling_y,
         ),
         [
+            pltpu.VMEM((1, count), jnp.int32),
             pltpu.VMEM((1, slots), jnp.int32),
-            space(slots, slots),
+            pltpu.VMEM((slots, slots), BF16),
+            pltpu.VMEM((slots, slots), BF16),
             block,
             block,
             block,
@@ -461,8 +537,8 @@
         ],
         scalars=1,
     )
-    cells, weight, *coefs, observed, live = on_chip(*outs[:7])
-    rows_next, cols_next, diag_next, rows_back, cols_back = outs[7:]
+    seeds, cells, high, low, *coefs, observed, live = on_chip(*outs[:9])
+    rows_next, cols_next, diag_next, rows_back, cols_back = outs[9:]
     above = shifted(rows_next, "gx", 1)
     corner = shifted_both(diag_next)
     left = shifted(cols_next, "gy", 1)
@@ -470,21 +546,22 @@
     right = shifted(cols_back, "gy", -1)
 
     probes, = on_chip(
-        *call(probes_kernel, (seeds,), [space(count, wide_rows, wide_cols)])
+        *call(probes_kernel, (seeds,), [space(count, *wide)])
     )
     image, sums, fix = call(
         image_kernel,
         (
             live,
             cells,
-            weight,
+            high,
+            low,
             *coefs,
             observed,
             *on_chip(above, left, corner, below, right),
             probes,
         ),
         [blocks, space(devices, 1, LANES), space(1, LANES)],
-        [space(wide_rows, wide_cols)] * 5,
+        [space(*wide)] * 4 + [space(count, *wide)] * 3,
     )
     sums = lax.all_to_all(sums, ("gx", "gy"), 0, 0, tiled=True)
     solved, trace = call(

time: 28.2 us -> 27.9 us (0.989)
  Pallas kernels: 5.64 us -> 4.82 us
  waiting for transfers between devices: 4.24 us -> 4.82 us
    pallas_call x4, Pallas kernels: 5.64 us -> 4.82 us  [call(): pl.pallas_call(kernel, out_shape=outs, in_specs=[SMEM] * scalars + [VMEM]...]
    ppermute x1, waiting for transfers between devices: 4.23 us -> 4.81 us  [shifted_both(): return lax.ppermute(value, ('gx', 'gy'), pairs)]
  transfers between devices with their start and end apart: 5 -> 5, of which waited for: 1 -> 1; matrix products, arithmetic and copies ran while one was open for 0% -> 0% of each run, Pallas kernels for 4% -> 1%
where the time goes in v4:
time: 27.9 us; the launch traced here: 27.8 us
  blocking collectives  9.21 us (33%)
  starting transfers between devices  7.59 us (27%)
  Pallas kernels  4.82 us (17%)
  waiting for transfers between devices  4.82 us (17%)
  between operations  1.31 us (5%)
    all_to_all x1, blocking collectives, per_device(): sums = lax.all_to_all(sums, ('gx', 'gy'), 0, 0, tiled=True)  9.21 us
    ppermute x4, starting transfers between devices, shifted(): return lax.ppermute(value, axis, pairs)  7.59 us
    pallas_call x4, Pallas kernels, call(): pl.pallas_call(kernel, out_shape=outs, in_specs=[SMEM] * scalars + [VMEM]...  4.82 us
    ppermute x1, waiting for transfers between devices, shifted_both(): return lax.ppermute(value, ('gx', 'gy'), pairs)  4.81 us
  transfers between devices with their start and end apart: 5, of which 1 were waited for; matrix products, arithmetic and copies ran while one was open for 0% of the time, Pallas kernels for 1%

profile of v4, /device:TPU:0, one launch (start us, length us, event | category | flops | bytes accessed | tf_op | source)
XLA Modules:
  0.0 27.8 jit_solution(4621845426383449212)
XLA Ops:
  1.3 1.7 %shard_map.86 = (s32[1,4]{1,0:T(1,128)S(1)}, s32[1,256]{1,0:T(1,128)S(1)}, bf16[256,256]{1,0:T(8,128)(2,1)S(1)}, bf16[256,256]{1,0:T(8,128)(2,1)S(1)}, f32[64,25...) custom-call(s32[1,1]{1,0:T(1,128)S(6)} %copy.9.number_ref, ...), custom_call_target="tpu_custom_call" | custom-call | tf_op jit(solution)/shard_map/pallas_call | solution.py:497
  3.0 3.0 %collective-permute-start = (f32[32,256]{1,0:T(8,128)S(1)}, f32[32,256]{1,0:T(8,128)S(1)}, u32[]{:S(2)}, u32[]{:S(2)}) collective-permute-start(f32[32,256]{1,0:T(8,128)S(1)} %get-tuple-element.29), channel_id=1, source_target_pairs={{0,4},{4,8},{8,12},{12,16},{16,20},{20,24},{24,28},{28,0},{1,5},{5... | collective-permute-start | bytes 98312 | tf_op jit(solution)/shard_map/ppermute | solution.py:20
  6.0 0.0 collective-permute-start.1
  6.0 3.2 %collective-permute-start.3 = (f32[8,256]{1,0:T(8,128)S(1)}, f32[8,256]{1,0:T(8,128)S(1)}, u32[]{:S(2)}, u32[]{:S(2)}) collective-permute-start(f32[8,256]{1,0:T(8,128)S(1)} %get-tuple-element.32), channel_id=1, source_target_pairs={{0,28},{4,0},{8,4},{12,8},{16,12},{20,16},{24,20},{28,24},{1,29},{... | collective-permute-start | bytes 24584 | tf_op jit(solution)/shard_map/ppermute | solution.py:20
  9.2 0.0 collective-permute-start.2
  9.2 1.4 %collective-permute-start.4 = (f32[8,128]{1,0:T(8,128)S(1)}, f32[8,128]{1,0:T(8,128)S(1)}, u32[]{:S(2)}, u32[]{:S(2)}) collective-permute-start(f32[8,128]{1,0:T(8,128)S(1)} %get-tuple-element.33), channel_id=1, source_target_pairs={{0,3},{1,0},{2,1},{3,2},{4,7},{5,4},{6,5},{7,6},{8,11},{9,8},{10,9... | collective-permute-start | bytes 12296 | tf_op jit(solution)/shard_map/ppermute | solution.py:20
  10.6 0.4 %shard_map.87.probes_ref = f32[4,3,96,128]{3,2,1,0:T(8,128)S(1)} custom-call(s32[1,4]{1,0:T(1,128)S(1)} %get-tuple-element.34.seeds_ref), custom_call_target="tpu_custom_call" | custom-call | tf_op jit(solution)/shard_map/pallas_call | solution.py:497
  11.0 4.8 %collective-permute-done.2.corner_ref = f32[8,128]{1,0:T(8,128)S(1)} collective-permute-done((f32[8,128]{1,0:T(8,128)S(1)}, f32[8,128]{1,0:T(8,128)S(1)}, u32[]{:S(2)}, u32[]{:S(2)}) %collective-permute-start.2) | collective-permute-done | bytes 4128 | tf_op jit(solution)/shard_map/ppermute | solution.py:30
  15.8 0.0 collective-permute-done.4.right_ref
  15.8 0.0 collective-permute-done.1.left_ref
  15.8 0.0 collective-permute-done.3.below_ref
  15.8 0.0 collective-permute-done.above_ref
  15.8 1.8 %shard_map.88 = (f32[4,64,256]{2,1,0:T(8,128)S(1)}, f32[32,1,128]{2,1,0:T(1,128)S(1)}, f32[1,128]{1,0:T(1,128)S(1)}) custom-call(f32[1,256]{1,0:T(1,128)S(1)} %get-tuple-element.21.live_ref, s32[1,256]{1,0:T(1,128)S(1)} %get-tuple-element.22.cells_ref, bf16[256,256]{1,0:T(8,128)(2,1)S(1)} %get-tuple-element.23.high_ref, ...), custom_call_target="tpu_custom_call" | custom-call | tf_op jit(solution)/shard_map/pallas_call | solution.py:497
  17.6 9.2 %all_to_all.5.sums_ref = f32[32,1,128]{2,1,0:T(1,128)S(1)} all-to-all(f32[32,1,128]{2,1,0:T(1,128)S(1)} %get-tuple-element.35), channel_id=1, replica_groups=mesh['gx'=8,'gy'=4] {'gx','gy'}, dimensions={0} | all-to-all | bytes 32768 | tf_op jit(solution)/shard_map/all_to_all | solution.py:566
  26.8 1.0 %shard_map.89 = (f32[4,64,256]{2,1,0:T(8,128)}, f32[1,1]{1,0:T(1,128)}) custom-call(f32[32,1,128]{2,1,0:T(1,128)S(1)} %all_to_all.5.sums_ref, f32[4,3,96,128]{3,2,1,0:T(8,128)S(1)} %shard_map.87.probes_ref, f32[4,64,256]{2,1,0:T(8,128)S(1)} %get-tuple-element.36.image_ref, f32[1,128]{1,0:T(1,128)S(1)} %get-tuple-element.37.fix_ref), custom_call_target="tpu_custom_call" | custom-call | tf_op jit(solution)/shard_map/pallas_call | solution.py:497
Async XLA Ops:
  3.0 12.8 %collective-permute-start = (f32[32,256]{1,0:T(8,128)S(1)}, f32[32,256]{1,0:T(8,128)S(1)}, u32[]{:S(2)}, u32[]{:S(2)}) collective-permute-start(f32[32,256]{1,0:T(8,128)S(1)} %get-tuple-element.29), channel_id=1, source_target_pairs={{0,4},{4,8},{8,12},{12,16},{16,20},{20,24},{24,28},{28,0},{1,5},{5... | collective-permute-start | bytes 98312 | tf_op jit(solution)/shard_map/ppermute | solution.py:20
  6.0 9.8 %collective-permute-start.1 = (f32[16,128]{1,0:T(8,128)S(1)}, f32[16,128]{1,0:T(8,128)S(1)}, u32[]{:S(2)}, u32[]{:S(2)}) collective-permute-start(f32[16,128]{1,0:T(8,128)S(1)} %get-tuple-element.30), channel_id=1, source_target_pairs={{0,1},{1,2},{2,3},{3,0},{4,5},{5,6},{6,7},{7,4},{8,9},{9,10},{10,1... | collective-permute-start | bytes 24584 | tf_op jit(solution)/shard_map/ppermute | solution.py:20
  6.0 9.8 %collective-permute-start.3 = (f32[8,256]{1,0:T(8,128)S(1)}, f32[8,256]{1,0:T(8,128)S(1)}, u32[]{:S(2)}, u32[]{:S(2)}) collective-permute-start(f32[8,256]{1,0:T(8,128)S(1)} %get-tuple-element.32), channel_id=1, source_target_pairs={{0,28},{4,0},{8,4},{12,8},{16,12},{20,16},{24,20},{28,24},{1,29},{... | collective-permute-start | bytes 24584 | tf_op jit(solution)/shard_map/ppermute | solution.py:20
  9.2 6.6 %collective-permute-start.2 = (f32[8,128]{1,0:T(8,128)S(1)}, f32[8,128]{1,0:T(8,128)S(1)}, u32[]{:S(2)}, u32[]{:S(2)}) collective-permute-start(f32[8,128]{1,0:T(8,128)S(1)} %get-tuple-element.31), channel_id=1, source_target_pairs={{0,5},{1,6},{2,7},{3,4},{4,9},{5,10},{6,11},{7,8},{8,13},{9,14},{1... | collective-permute-start | bytes 12296 | tf_op jit(solution)/shard_map/ppermute | solution.py:30
  9.2 6.6 %collective-permute-start.4 = (f32[8,128]{1,0:T(8,128)S(1)}, f32[8,128]{1,0:T(8,128)S(1)}, u32[]{:S(2)}, u32[]{:S(2)}) collective-permute-start(f32[8,128]{1,0:T(8,128)S(1)} %get-tuple-element.33), channel_id=1, source_target_pairs={{0,3},{1,0},{2,1},{3,2},{4,7},{5,4},{6,5},{7,6},{8,11},{9,8},{10,9... | collective-permute-start | bytes 12296 | tf_op jit(solution)/shard_map/ppermute | solution.py:20

commit v5 on v4

--- a/solution.py
+++ b/solution.py
@@ -14,9 +14,9 @@
 VMEM = pl.BlockSpec(memory_space=pltpu.VMEM)
 
 
-def shifted(value, axis, steps):
+def swapped(value, axis, odd_first):
     count = lax.axis_size(axis)
-    pairs = [(source, (source + steps) % count) for source in range(count)]
+    pairs = [(i, (i + (1 if i % 2 == odd_first else -1)) % count) for i in range(count)]
     return lax.ppermute(value, axis, pairs)
 
 
@@ -157,13 +157,12 @@
     last = slice(block_cols - LANES, block_cols)
 
     sub = iota((SUBS, block_cols), 0)
-    rows_next_ref[:SUBS] = cx[tail]
-    rows_next_ref[SUBS : 2 * SUBS] = jnp.where(sub >= 4, d[tail], roll(cy[tail], -4, 0))
+    onward = [cx[tail], jnp.where(sub >= 4, d[tail], roll(cy[tail], -4, 0))]
     for k in range(0, count, 2):
         tile = observed[k][tail]
         if k + 1 < count:
             tile = jnp.where(sub >= 5, tile, roll(observed[k + 1][tail], -3, 0))
-        rows_next_ref[(2 + k // 2) * SUBS : (3 + k // 2) * SUBS] = tile
+        onward.append(tile)
 
     lane = iota((block_rows, LANES), 1)
     side = jnp.where(lane >= LANES - 5, cy[:, last], roll(d[:, last], -5, 1))
@@ -171,7 +170,7 @@
     for k in range(count):
         edge = LANES - 13 - 3 * k
         side = jnp.where(lane >= edge, side, roll(observed[k][:, last], edge, 1))
-    cols_next_ref[...] = compact(side, side_width(count))
+    cols_onward = compact(side, side_width(count))
 
     lane = iota((SUBS, LANES), 1)
     corner = d[tail, last]
@@ -180,13 +179,25 @@
         corner = jnp.where(lane >= edge, corner, roll(value[tail, last], edge, 1))
     diag_next_ref[...] = corner
 
-    rows_back_ref[...] = jnp.where(
+    back = jnp.where(
         sub == 0, cx[:SUBS], jnp.where(sub == 1, roll(d[:SUBS], 1, 0), roll(cy[:SUBS], 2, 0))
     )
+    odd = lax.rem(lax.axis_index("gx"), 2) == 1
+    rows_next_ref[:SUBS] = jnp.where(odd, onward[0], back)
+    rows_back_ref[:SUBS] = jnp.where(odd, back, onward[0])
+    for i in range(1, len(onward)):
+        rows_next_ref[i * SUBS : (i + 1) * SUBS] = onward[i]
+        rows_back_ref[i * SUBS : (i + 1) * SUBS] = onward[i]
     lane = iota((block_rows, LANES), 1)
     back = jnp.where(lane == LANES - 1, roll(cy[:, :LANES], -1, 1), roll(d[:, :LANES], -2, 1))
     back = jnp.where(lane >= LANES - 2, back, roll(cx[:, :LANES], -3, 1))
-    cols_back_ref[...] = compact(back, BACK_WIDTH)
+    cols_back = compact(back, BACK_WIDTH)
+    size = cols_back.shape[0]
+    odd = lax.rem(lax.axis_index("gy"), 2) == 1
+    cols_next_ref[...] = cols_onward
+    cols_back_ref[...] = cols_onward
+    cols_next_ref[:size] = jnp.where(odd, cols_onward[:size], cols_back)
+    cols_back_ref[:size] = jnp.where(odd, cols_back, cols_onward[:size])
 
 
 TOP = 2 * SUBS
@@ -228,7 +239,7 @@
 
 def image_kernel(
     live_ref, cells_ref, high_ref, low_ref, d_ref, cx_ref, cy_ref, obs_ref,
-    above_ref, left_ref, corner_ref, below_ref, right_ref, probes_ref,
+    rows_a_ref, rows_b_ref, cols_a_ref, cols_b_ref, corner_ref, probes_ref,
     image_ref, sums_ref, fix_ref,
     centre, cx_wide, cy_wide, cy_before, seen, once, image,
 ):
@@ -237,11 +248,15 @@
     side = tiles - 1
     own = slice(TOP, TOP + block_rows)
     over, under = slice(TOP - SUBS, TOP), slice(TOP + block_rows, TOP + block_rows + SUBS)
-    left = expand(left_ref[...], block_rows, side_width(count))
-    right = expand(right_ref[...], block_rows, BACK_WIDTH)
+    odd = lax.rem(lax.axis_index("gy"), 2) == 1
+    cols_a, cols_b = cols_a_ref[...], cols_b_ref[...]
+    left = expand(jnp.where(odd, cols_a, cols_b), block_rows, side_width(count))
+    right = expand(jnp.where(odd, cols_b, cols_a), block_rows, BACK_WIDTH)
     corner = corner_ref[...]
+    odd = lax.rem(lax.axis_index("gx"), 2) == 1
+    above_ref = jnp.where(odd, rows_a_ref[...], rows_b_ref[...])
     above = above_ref[SUBS : 2 * SUBS]
-    below = below_ref[...]
+    below = jnp.where(odd, rows_b_ref[:SUBS], rows_a_ref[:SUBS])
     lane = iota((block_rows, LANES), 1)
     sub, tile_lane = iota((SUBS, LANES), 0), iota((SUBS, LANES), 1)
     nothing = jnp.zeros((SUBS, LANES), F32)
@@ -532,18 +547,18 @@
             space(SUBS * (2 + (count + 1) // 2), block_cols),
             space(compact_rows(block_rows, side_width(count)), LANES),
             space(SUBS, LANES),
-            space(SUBS, block_cols),
-            space(compact_rows(block_rows, BACK_WIDTH), LANES),
+            space(SUBS * (2 + (count + 1) // 2), block_cols),
+            space(compact_rows(block_rows, side_width(count)), LANES),
         ],
         scalars=1,
     )
     seeds, cells, high, low, *coefs, observed, live = on_chip(*outs[:9])
     rows_next, cols_next, diag_next, rows_back, cols_back = outs[9:]
-    above = shifted(rows_next, "gx", 1)
+    rows_b = swapped(rows_next, "gx", 1)
+    rows_a = swapped(rows_back, "gx", 0)
     corner = shifted_both(diag_next)
-    left = shifted(cols_next, "gy", 1)
-    below = shifted(rows_back, "gx", -1)
-    right = shifted(cols_back, "gy", -1)
+    cols_b = swapped(cols_next, "gy", 1)
+    cols_a = swapped(cols_back, "gy", 0)
 
     probes, = on_chip(
         *call(probes_kernel, (seeds,), [space(count, *wide)])
@@ -557,7 +572,7 @@
             low,
             *coefs,
             observed,
-            *on_chip(above, left, corner, below, right),
+            *on_chip(rows_a, rows_b, cols_a, cols_b, corner),
             probes,
         ),
         [blocks, space(devices, 1, LANES), space(1, LANES)],

time: 27.9 us -> 29.6 us (1.061)
  waiting for transfers between devices: 4.82 us -> 6.22 us
  starting transfers between devices: 7.59 us -> 8.24 us
  blocking collectives: 9.21 us -> 8.87 us
    ppermute x1, waiting for transfers between devices: 4.81 us -> 6.21 us  [shifted_both(): return lax.ppermute(value, ('gx', 'gy'), pairs)]
    ppermute x4, starting transfers between devices: 7.59 us -> 8.24 us  [swapped(): return lax.ppermute(value, axis, pairs)]
    all_to_all x1, blocking collectives: 9.21 us -> 8.87 us  [per_device(): sums = lax.all_to_all(sums, ('gx', 'gy'), 0, 0, tiled=True)]
where the time goes in v5:
time: 29.6 us; the launch traced here: 29.4 us
  blocking collectives  8.87 us (30%)
  starting transfers between devices  8.24 us (28%)
  waiting for transfers between devices  6.22 us (21%)
  Pallas kernels  4.73 us (16%)
  between operations  1.32 us (4%)
    all_to_all x1, blocking collectives, per_device(): sums = lax.all_to_all(sums, ('gx', 'gy'), 0, 0, tiled=True)  8.87 us
    ppermute x4, starting transfers between devices, swapped(): return lax.ppermute(value, axis, pairs)  8.24 us
    ppermute x1, waiting for transfers between devices, shifted_both(): return lax.ppermute(value, ('gx', 'gy'), pairs)  6.21 us
    pallas_call x4, Pallas kernels, call(): pl.pallas_call(kernel, out_shape=outs, in_specs=[SMEM] * scalars + [VMEM]...  4.73 us
  transfers between devices with their start and end apart: 5, of which 1 were waited for; matrix products, arithmetic and copies ran while one was open for 0% of the time, Pallas kernels for 1%

profile of v5, /device:TPU:0, one launch (start us, length us, event | category | flops | bytes accessed | tf_op | source)
XLA Modules:
  0.0 29.4 jit_solution(10720584439416341148)
XLA Ops:
  1.3 1.7 %shard_map.86 = (s32[1,4]{1,0:T(1,128)S(1)}, s32[1,256]{1,0:T(1,128)S(1)}, bf16[256,256]{1,0:T(8,128)(2,1)S(1)}, bf16[256,256]{1,0:T(8,128)(2,1)S(1)}, f32[64,25...) custom-call(s32[1,1]{1,0:T(1,128)S(6)} %copy.9.number_ref, ...), custom_call_target="tpu_custom_call" | custom-call | tf_op jit(solution)/shard_map/pallas_call | solution.py:512
  3.0 3.0 %collective-permute-start = (f32[32,256]{1,0:T(8,128)S(1)}, f32[32,256]{1,0:T(8,128)S(1)}, u32[]{:S(2)}, u32[]{:S(2)}) collective-permute-start(f32[32,256]{1,0:T(8,128)S(1)} %get-tuple-element.29), channel_id=1, source_target_pairs={{0,4},{4,0},{8,12},{12,8},{16,20},{20,16},{24,28},{28,24},{1,5},{5... | collective-permute-start | bytes 98312 | tf_op jit(solution)/shard_map/ppermute | solution.py:20
  6.0 3.6 %collective-permute-start.1 = (f32[32,256]{1,0:T(8,128)S(1)}, f32[32,256]{1,0:T(8,128)S(1)}, u32[]{:S(2)}, u32[]{:S(2)}) collective-permute-start(f32[32,256]{1,0:T(8,128)S(1)} %get-tuple-element.30), channel_id=1, source_target_pairs={{0,28},{4,8},{8,4},{12,16},{16,12},{20,24},{24,20},{28,0},{1,29},{... | collective-permute-start | bytes 98312 | tf_op jit(solution)/shard_map/ppermute | solution.py:20
  9.6 0.0 collective-permute-start.2
  9.6 1.6 %collective-permute-start.3 = (f32[16,128]{1,0:T(8,128)S(1)}, f32[16,128]{1,0:T(8,128)S(1)}, u32[]{:S(2)}, u32[]{:S(2)}) collective-permute-start(f32[16,128]{1,0:T(8,128)S(1)} %get-tuple-element.32), channel_id=1, source_target_pairs={{0,3},{1,2},{2,1},{3,0},{4,7},{5,6},{6,5},{7,4},{8,11},{9,10},{10,... | collective-permute-start | bytes 24584 | tf_op jit(solution)/shard_map/ppermute | solution.py:20
  11.2 0.0 collective-permute-start.4
  11.2 0.4 %shard_map.87.probes_ref = f32[4,3,96,128]{3,2,1,0:T(8,128)S(1)} custom-call(s32[1,4]{1,0:T(1,128)S(1)} %get-tuple-element.34.seeds_ref), custom_call_target="tpu_custom_call" | custom-call | tf_op jit(solution)/shard_map/pallas_call | solution.py:512
  11.6 6.2 %collective-permute-done.4.corner_ref = f32[8,128]{1,0:T(8,128)S(1)} collective-permute-done((f32[8,128]{1,0:T(8,128)S(1)}, f32[8,128]{1,0:T(8,128)S(1)}, u32[]{:S(2)}, u32[]{:S(2)}) %collective-permute-start.4) | collective-permute-done | bytes 4128 | tf_op jit(solution)/shard_map/ppermute | solution.py:30
  17.8 0.0 collective-permute-done.2.cols_a_ref
  17.8 0.0 collective-permute-done.3.cols_b_ref
  17.8 0.0 collective-permute-done.rows_a_ref
  17.9 0.0 collective-permute-done.1.rows_b_ref
  17.9 1.7 %shard_map.88 = (f32[4,64,256]{2,1,0:T(8,128)S(1)}, f32[32,1,128]{2,1,0:T(1,128)S(1)}, f32[1,128]{1,0:T(1,128)S(1)}) custom-call(f32[1,256]{1,0:T(1,128)S(1)} %get-tuple-element.21.live_ref, s32[1,256]{1,0:T(1,128)S(1)} %get-tuple-element.22.cells_ref, bf16[256,256]{1,0:T(8,128)(2,1)S(1)} %get-tuple-element.23.high_ref, ...), custom_call_target="tpu_custom_call" | custom-call | tf_op jit(solution)/shard_map/pallas_call | solution.py:512
  19.6 8.9 %all_to_all.5.sums_ref = f32[32,1,128]{2,1,0:T(1,128)S(1)} all-to-all(f32[32,1,128]{2,1,0:T(1,128)S(1)} %get-tuple-element.35), channel_id=1, replica_groups=mesh['gx'=8,'gy'=4] {'gx','gy'}, dimensions={0} | all-to-all | bytes 32768 | tf_op jit(solution)/shard_map/all_to_all | solution.py:581
  28.4 1.0 %shard_map.89 = (f32[4,64,256]{2,1,0:T(8,128)}, f32[1,1]{1,0:T(1,128)}) custom-call(f32[32,1,128]{2,1,0:T(1,128)S(1)} %all_to_all.5.sums_ref, f32[4,3,96,128]{3,2,1,0:T(8,128)S(1)} %shard_map.87.probes_ref, f32[4,64,256]{2,1,0:T(8,128)S(1)} %get-tuple-element.36.image_ref, f32[1,128]{1,0:T(1,128)S(1)} %get-tuple-element.37.fix_ref), custom_call_target="tpu_custom_call" | custom-call | tf_op jit(solution)/shard_map/pallas_call | solution.py:512
Async XLA Ops:
  3.0 14.9 %collective-permute-start = (f32[32,256]{1,0:T(8,128)S(1)}, f32[32,256]{1,0:T(8,128)S(1)}, u32[]{:S(2)}, u32[]{:S(2)}) collective-permute-start(f32[32,256]{1,0:T(8,128)S(1)} %get-tuple-element.29), channel_id=1, source_target_pairs={{0,4},{4,0},{8,12},{12,8},{16,20},{20,16},{24,28},{28,24},{1,5},{5... | collective-permute-start | bytes 98312 | tf_op jit(solution)/shard_map/ppermute | solution.py:20
  6.0 11.9 %collective-permute-start.1 = (f32[32,256]{1,0:T(8,128)S(1)}, f32[32,256]{1,0:T(8,128)S(1)}, u32[]{:S(2)}, u32[]{:S(2)}) collective-permute-start(f32[32,256]{1,0:T(8,128)S(1)} %get-tuple-element.30), channel_id=1, source_target_pairs={{0,28},{4,8},{8,4},{12,16},{16,12},{20,24},{24,20},{28,0},{1,29},{... | collective-permute-start | bytes 98312 | tf_op jit(solution)/shard_map/ppermute | solution.py:20
  9.6 8.3 %collective-permute-start.2 = (f32[16,128]{1,0:T(8,128)S(1)}, f32[16,128]{1,0:T(8,128)S(1)}, u32[]{:S(2)}, u32[]{:S(2)}) collective-permute-start(f32[16,128]{1,0:T(8,128)S(1)} %get-tuple-element.31), channel_id=1, source_target_pairs={{0,1},{1,0},{2,3},{3,2},{4,5},{5,4},{6,7},{7,6},{8,9},{9,8},{10,11... | collective-permute-start | bytes 24584 | tf_op jit(solution)/shard_map/ppermute | solution.py:20
  9.6 8.3 %collective-permute-start.3 = (f32[16,128]{1,0:T(8,128)S(1)}, f32[16,128]{1,0:T(8,128)S(1)}, u32[]{:S(2)}, u32[]{:S(2)}) collective-permute-start(f32[16,128]{1,0:T(8,128)S(1)} %get-tuple-element.32), channel_id=1, source_target_pairs={{0,3},{1,2},{2,1},{3,0},{4,7},{5,6},{6,5},{7,4},{8,11},{9,10},{10,... | collective-permute-start | bytes 24584 | tf_op jit(solution)/shard_map/ppermute | solution.py:20
  11.2 6.6 %collective-permute-start.4 = (f32[8,128]{1,0:T(8,128)S(1)}, f32[8,128]{1,0:T(8,128)S(1)}, u32[]{:S(2)}, u32[]{:S(2)}) collective-permute-start(f32[8,128]{1,0:T(8,128)S(1)} %get-tuple-element.33), channel_id=1, source_target_pairs={{0,5},{1,6},{2,7},{3,4},{4,9},{5,10},{6,11},{7,8},{8,13},{9,14},{1... | collective-permute-start | bytes 12296 | tf_op jit(solution)/shard_map/ppermute | solution.py:30

commit v6 on v5

--- a/solution.py
+++ b/solution.py
@@ -203,7 +203,7 @@
 TOP = 2 * SUBS
 
 
-def probes_kernel(seeds_ref, probes_ref):
+def probes_kernel(seeds_ref, cells_ref, probes_ref, row_hot_ref, col_hot_ref):
     count, tiles, wide_rows, _ = probes_ref.shape
     block_rows, block_cols = wide_rows - 2 * TOP, (tiles - 1) * LANES
     row_start = lax.axis_index("gx") * block_rows
@@ -224,6 +224,8 @@
         col_ids = jnp.where(col_ids >= cols_total, col_ids - cols_total, col_ids)
         for k in range(count):
             probes_ref[k, j] = sign_bits(seeds_ref[:, k : k + 1], row_ids, col_ids)
+    row_hot, col_hot = one_hots(cells_ref[...], block_rows, block_cols)
+    row_hot_ref[...], col_hot_ref[...] = row_hot, col_hot
 
 
 def side_step(tiles, steps):
@@ -240,7 +242,7 @@
 def image_kernel(
     live_ref, cells_ref, high_ref, low_ref, d_ref, cx_ref, cy_ref, obs_ref,
     rows_a_ref, rows_b_ref, cols_a_ref, cols_b_ref, corner_ref, probes_ref,
-    image_ref, sums_ref, fix_ref,
+    row_hot_ref, col_hot_ref, image_ref, sums_ref, fix_ref,
     centre, cx_wide, cy_wide, cy_before, seen, once, image,
 ):
     count, block_rows, block_cols = obs_ref.shape
@@ -283,7 +285,6 @@
         tile = above_ref[(2 + k // 2) * SUBS : (3 + k // 2) * SUBS]
         tile = roll(tile, 3, 0) if k % 2 else tile
         for j in range(side):
-            seen[k, j, own] = obs_ref[k, :, lanes_of(j)]
             seen[k, j, over] = jnp.where(sub >= SUBS - 3, tile[:, lanes_of(j)], 0.0)
         seen[k, side, own] = jnp.where(lane >= LANES - 3, roll(left, 13 + 3 * k, 1), 0.0)
         tile = roll(corner, HALO * (3 + k), 1)
@@ -347,7 +348,11 @@
         for k in range(count):
             result, _ = stencil(once, k, start, coefs)
             for j in range(tiles):
-                image[k, j, rows_at(start)] = result[j] + seen[k, j, rows_at(start)]
+                if j == side or start < TOP:
+                    added = seen[k, j, rows_at(start)]
+                else:
+                    added = obs_ref[k, rows_at(start, -TOP), lanes_of(j)]
+                image[k, j, rows_at(start)] = result[j] + added
         return carry
 
     def products(start):
@@ -382,7 +387,7 @@
 
     slots = cells_ref.shape[1]
     cells = cells_ref[...]
-    row_hot, col_hot = one_hots(cells, block_rows, block_cols)
+    row_hot, col_hot = row_hot_ref[...], col_hot_ref[...]
     live = live_ref[...]
     stack, first_miss, second_miss = [], [], []
     for k in range(count):
@@ -560,8 +565,12 @@
     cols_b = swapped(cols_next, "gy", 1)
     cols_a = swapped(cols_back, "gy", 0)
 
-    probes, = on_chip(
-        *call(probes_kernel, (seeds,), [space(count, *wide)])
+    probes, row_hot, col_hot = on_chip(
+        *call(
+            probes_kernel,
+            (seeds, cells),
+            [space(count, *wide), space(block_rows, slots), pltpu.VMEM((block_cols, slots), BF16)],
+        )
     )
     image, sums, fix = call(
         image_kernel,
@@ -574,6 +583,8 @@
             observed,
             *on_chip(rows_a, rows_b, cols_a, cols_b, corner),
             probes,
+            row_hot,
+            col_hot,
         ),
         [blocks, space(devices, 1, LANES), space(1, LANES)],
         [space(*wide)] * 4 + [space(count, *wide)] * 3,

time: 29.6 us -> 29.6 us (level)
  transfers between devices with their start and end apart: 5 -> 5, of which waited for: 1 -> 1; matrix products, arithmetic and copies ran while one was open for 0% -> 0% of each run, Pallas kernels for 1% -> 2%
where the time goes in v6:
time: 29.6 us; the launch traced here: 29.4 us
  blocking collectives  8.87 us (30%)
  starting transfers between devices  8.24 us (28%)
  waiting for transfers between devices  6.17 us (21%)
  Pallas kernels  4.83 us (16%)
  between operations  1.31 us (4%)
    all_to_all x1, blocking collectives, per_device(): sums = lax.all_to_all(sums, ('gx', 'gy'), 0, 0, tiled=True)  8.87 us
    ppermute x4, starting transfers between devices, swapped(): return lax.ppermute(value, axis, pairs)  8.24 us
    ppermute x1, waiting for transfers between devices, shifted_both(): return lax.ppermute(value, ('gx', 'gy'), pairs)  6.16 us
    pallas_call x4, Pallas kernels, call(): pl.pallas_call(kernel, out_shape=outs, in_specs=[SMEM] * scalars + [VMEM]...  4.83 us
  transfers between devices with their start and end apart: 5, of which 1 were waited for; matrix products, arithmetic and copies ran while one was open for 0% of the time, Pallas kernels for 2%

profile of v6, /device:TPU:0, one launch (start us, length us, event | category | flops | bytes accessed | tf_op | source)
XLA Modules:
  0.0 29.4 jit_solution(1565330449597761375)
XLA Ops:
  1.3 1.7 %shard_map.86 = (s32[1,4]{1,0:T(1,128)S(1)}, s32[1,256]{1,0:T(1,128)S(1)}, bf16[256,256]{1,0:T(8,128)(2,1)S(1)}, bf16[256,256]{1,0:T(8,128)(2,1)S(1)}, f32[64,25...) custom-call(s32[1,1]{1,0:T(1,128)S(6)} %copy.9.number_ref, ...), custom_call_target="tpu_custom_call" | custom-call | tf_op jit(solution)/shard_map/pallas_call | solution.py:517
  3.0 3.0 %collective-permute-start = (f32[32,256]{1,0:T(8,128)S(1)}, f32[32,256]{1,0:T(8,128)S(1)}, u32[]{:S(2)}, u32[]{:S(2)}) collective-permute-start(f32[32,256]{1,0:T(8,128)S(1)} %get-tuple-element.32), channel_id=1, source_target_pairs={{0,4},{4,0},{8,12},{12,8},{16,20},{20,16},{24,28},{28,24},{1,5},{5... | collective-permute-start | bytes 98312 | tf_op jit(solution)/shard_map/ppermute | solution.py:20
  6.0 3.6 %collective-permute-start.1 = (f32[32,256]{1,0:T(8,128)S(1)}, f32[32,256]{1,0:T(8,128)S(1)}, u32[]{:S(2)}, u32[]{:S(2)}) collective-permute-start(f32[32,256]{1,0:T(8,128)S(1)} %get-tuple-element.33), channel_id=1, source_target_pairs={{0,28},{4,8},{8,4},{12,16},{16,12},{20,24},{24,20},{28,0},{1,29},{... | collective-permute-start | bytes 98312 | tf_op jit(solution)/shard_map/ppermute | solution.py:20
  9.6 0.0 collective-permute-start.2
  9.6 1.6 %collective-permute-start.3 = (f32[16,128]{1,0:T(8,128)S(1)}, f32[16,128]{1,0:T(8,128)S(1)}, u32[]{:S(2)}, u32[]{:S(2)}) collective-permute-start(f32[16,128]{1,0:T(8,128)S(1)} %get-tuple-element.35), channel_id=1, source_target_pairs={{0,3},{1,2},{2,1},{3,0},{4,7},{5,6},{6,5},{7,4},{8,11},{9,10},{10,... | collective-permute-start | bytes 24584 | tf_op jit(solution)/shard_map/ppermute | solution.py:20
  11.2 0.0 collective-permute-start.4
  11.2 0.5 %shard_map.87 = (f32[4,3,96,128]{3,2,1,0:T(8,128)S(1)}, f32[64,256]{1,0:T(8,128)S(1)}, bf16[256,256]{1,0:T(8,128)(2,1)S(1)}) custom-call(s32[1,4]{1,0:T(1,128)S(1)} %get-tuple-element.37.seeds_ref, s32[1,256]{1,0:T(1,128)S(1)} %get-tuple-element.25.cells_ref), custom_call_target="tpu_custom_call" | custom-call | tf_op jit(solution)/shard_map/pallas_call | solution.py:517
  11.7 6.2 %collective-permute-done.4.corner_ref = f32[8,128]{1,0:T(8,128)S(1)} collective-permute-done((f32[8,128]{1,0:T(8,128)S(1)}, f32[8,128]{1,0:T(8,128)S(1)}, u32[]{:S(2)}, u32[]{:S(2)}) %collective-permute-start.4) | collective-permute-done | bytes 4128 | tf_op jit(solution)/shard_map/ppermute | solution.py:30
  17.8 0.0 collective-permute-done.2.cols_a_ref
  17.8 0.0 collective-permute-done.3.cols_b_ref
  17.8 0.0 collective-permute-done.rows_a_ref
  17.9 0.0 collective-permute-done.1.rows_b_ref
  17.9 1.7 %shard_map.88 = (f32[4,64,256]{2,1,0:T(8,128)S(1)}, f32[32,1,128]{2,1,0:T(1,128)S(1)}, f32[1,128]{1,0:T(1,128)S(1)}) custom-call(f32[1,256]{1,0:T(1,128)S(1)} %get-tuple-element.24.live_ref, s32[1,256]{1,0:T(1,128)S(1)} %get-tuple-element.25.cells_ref, bf16[256,256]{1,0:T(8,128)(2,1)S(1)} %get-tuple-element.26.high_ref, ...), custom_call_target="tpu_custom_call" | custom-call | tf_op jit(solution)/shard_map/pallas_call | solution.py:517
  19.6 8.9 %all_to_all.5.sums_ref = f32[32,1,128]{2,1,0:T(1,128)S(1)} all-to-all(f32[32,1,128]{2,1,0:T(1,128)S(1)} %get-tuple-element.41), channel_id=1, replica_groups=mesh['gx'=8,'gy'=4] {'gx','gy'}, dimensions={0} | all-to-all | bytes 32768 | tf_op jit(solution)/shard_map/all_to_all | solution.py:592
  28.5 1.0 %shard_map.89 = (f32[4,64,256]{2,1,0:T(8,128)}, f32[1,1]{1,0:T(1,128)}) custom-call(f32[32,1,128]{2,1,0:T(1,128)S(1)} %all_to_all.5.sums_ref, f32[4,3,96,128]{3,2,1,0:T(8,128)S(1)} %get-tuple-element.38.probes_ref, f32[4,64,256]{2,1,0:T(8,128)S(1)} %get-tuple-element.42.image_ref, f32[1,128]{1,0:T(1,128)S(1)} %get-tuple-element.43.fix_ref), custom_call_target="tpu_custom_call" | custom-call | tf_op jit(solution)/shard_map/pallas_call | solution.py:517
Async XLA Ops:
  3.0 14.9 %collective-permute-start = (f32[32,256]{1,0:T(8,128)S(1)}, f32[32,256]{1,0:T(8,128)S(1)}, u32[]{:S(2)}, u32[]{:S(2)}) collective-permute-start(f32[32,256]{1,0:T(8,128)S(1)} %get-tuple-element.32), channel_id=1, source_target_pairs={{0,4},{4,0},{8,12},{12,8},{16,20},{20,16},{24,28},{28,24},{1,5},{5... | collective-permute-start | bytes 98312 | tf_op jit(solution)/shard_map/ppermute | solution.py:20
  6.0 11.9 %collective-permute-start.1 = (f32[32,256]{1,0:T(8,128)S(1)}, f32[32,256]{1,0:T(8,128)S(1)}, u32[]{:S(2)}, u32[]{:S(2)}) collective-permute-start(f32[32,256]{1,0:T(8,128)S(1)} %get-tuple-element.33), channel_id=1, source_target_pairs={{0,28},{4,8},{8,4},{12,16},{16,12},{20,24},{24,20},{28,0},{1,29},{... | collective-permute-start | bytes 98312 | tf_op jit(solution)/shard_map/ppermute | solution.py:20
  9.6 8.3 %collective-permute-start.2 = (f32[16,128]{1,0:T(8,128)S(1)}, f32[16,128]{1,0:T(8,128)S(1)}, u32[]{:S(2)}, u32[]{:S(2)}) collective-permute-start(f32[16,128]{1,0:T(8,128)S(1)} %get-tuple-element.34), channel_id=1, source_target_pairs={{0,1},{1,0},{2,3},{3,2},{4,5},{5,4},{6,7},{7,6},{8,9},{9,8},{10,11... | collective-permute-start | bytes 24584 | tf_op jit(solution)/shard_map/ppermute | solution.py:20
  9.6 8.3 %collective-permute-start.3 = (f32[16,128]{1,0:T(8,128)S(1)}, f32[16,128]{1,0:T(8,128)S(1)}, u32[]{:S(2)}, u32[]{:S(2)}) collective-permute-start(f32[16,128]{1,0:T(8,128)S(1)} %get-tuple-element.35), channel_id=1, source_target_pairs={{0,3},{1,2},{2,1},{3,0},{4,7},{5,6},{6,5},{7,4},{8,11},{9,10},{10,... | collective-permute-start | bytes 24584 | tf_op jit(solution)/shard_map/ppermute | solution.py:20
  11.2 6.6 %collective-permute-start.4 = (f32[8,128]{1,0:T(8,128)S(1)}, f32[8,128]{1,0:T(8,128)S(1)}, u32[]{:S(2)}, u32[]{:S(2)}) collective-permute-start(f32[8,128]{1,0:T(8,128)S(1)} %get-tuple-element.36), channel_id=1, source_target_pairs={{0,5},{1,6},{2,7},{3,4},{4,9},{5,10},{6,11},{7,8},{8,13},{9,14},{1... | collective-permute-start | bytes 12296 | tf_op jit(solution)/shard_map/ppermute | solution.py:30
